TPU v7x, 32 devices: a whole 2x2x4 slice. The times are simulated.
32 devices in a mesh: samples: 4 (over y, x), features: 4 (over z), rhs: 2 (over core).
Axes of the slice: x: 2, y: 2, z: 4, core: 2. Of those that a mesh axis runs over, the one named last changes fastest.
Arguments:
- design: bfloat16 [32768, 32768], P(('samples', 'rhs'), 'features'), may hold values from -0.03125 to 0.03125
- right_side: float32 [32768, 64], P('features', 'rhs'), may hold values from -6 to 6
- factor: bfloat16 [32768, 768], P('features', 'rhs'), may hold values from -0.03125 to 0.03125
- nystrom_values: float32 [768], replicated, may hold values from 0.5 to 3
Outputs:
- solution: float32 [32768, 64], P('features', 'rhs')
- residual: float32 [32768, 64], P('features', 'rhs')
All inputs are finite; a program needn't handle non-finite values.
Results may differ from a plain program's by a relative error of at most 0.0181.
Values may be sent and summed in bfloat16 or wider, within the bound.
No kernel may reach another device: no remote copies, remote signals or barrier semaphores. Data moves between devices by JAX's collectives and lax.ppermute only.
A program may use at most 192 MiB of HBM per device.

v0:
```python
import jax
import jax.numpy as jnp
from jax import lax
from jax.sharding import PartitionSpec as P

ITERS = 3


ridge_weight = 1.0


def inner_prod(left, right):
    return lax.dot_general(
        left,
        right,
        (((0,), (0,)), ((), ())),
        precision=lax.Precision.HIGHEST,
        preferred_element_type=jnp.float32,
    )


def split_parts(values):
    upper = values.astype(jnp.bfloat16)
    widened = lax.optimization_barrier(upper).astype(jnp.float32)
    lower = (values - widened).astype(jnp.bfloat16)
    return (upper, lower)


def factor_inner(factor_narrow, values):
    upper, lower = split_parts(values)
    dims = (((0,), (0,)), ((), ()))
    first = lax.dot_general(factor_narrow, upper, dims, preferred_element_type=jnp.float32)
    second = lax.dot_general(factor_narrow, lower, dims, preferred_element_type=jnp.float32)
    return first + second


def factor_times(factor_narrow, values):
    upper, lower = split_parts(values)
    first = jnp.dot(factor_narrow, upper, preferred_element_type=jnp.float32)
    second = jnp.dot(factor_narrow, lower, preferred_element_type=jnp.float32)
    return first + second


def shards(design, right_side, factor, nystrom_values):
    feat_rows, col_share = right_side.shape
    shrink = (1.0 + jnp.min(nystrom_values)) / (1.0 + nystrom_values) - 1.0
    columns = lax.all_gather(right_side, "rhs", axis=1, tiled=True)
    residual = columns
    basis_rows = lax.all_gather(factor, "rhs", axis=1, tiled=True)

    def totals(values):
        return lax.psum(values, "features")

    def expand(projected):
        return factor_times(basis_rows, shrink[:, None] * projected)

    projected = totals(factor_inner(basis_rows, residual))
    direction = residual + expand(projected)
    solution = jnp.zeros_like(residual)
    for iteration in range(ITERS):
        narrow = direction.astype(jnp.bfloat16)
        apply_partial_value = jnp.dot(design, narrow, preferred_element_type=jnp.float32)
        narrow_images = lax.psum(apply_partial_value, "features").astype(jnp.bfloat16)
        feature_term = lax.dot_general(
            design, narrow_images, (((0,), (0,)), ((), ())), preferred_element_type=jnp.float32
        )
        summed = lax.psum(feature_term, ("samples", "rhs"))
        applied = summed + ridge_weight * direction
        gram_block, cross_term, image_res, image_image, factor_image = totals(
            (
                inner_prod(direction, applied),
                inner_prod(direction, residual),
                inner_prod(applied, residual),
                inner_prod(applied, applied),
                factor_inner(basis_rows, applied),
            )
        )
        gram_block = 0.5 * (gram_block + gram_block.T)
        chol_lower = jnp.linalg.cholesky(gram_block)
        unit_dir = jax.scipy.linalg.solve_triangular(chol_lower, direction.T, lower=True).T
        unit_img = jax.scipy.linalg.solve_triangular(chol_lower, applied.T, lower=True).T
        step_coef = jax.scipy.linalg.solve_triangular(chol_lower, cross_term, lower=True)
        solution = solution + jnp.dot(unit_dir, step_coef, precision=lax.Precision.HIGHEST)
        residual = residual - jnp.dot(unit_img, step_coef, precision=lax.Precision.HIGHEST)
        if iteration + 1 < ITERS:
            back_step = jax.scipy.linalg.solve_triangular(
                chol_lower, step_coef, lower=True, trans=1
            )
            projected = projected - jnp.dot(
                factor_image, back_step, precision=lax.Precision.HIGHEST
            )
            scaled = residual + expand(projected)
            image_new = image_res - jnp.dot(image_image, back_step, precision=lax.Precision.HIGHEST)
            image_new = image_new + inner_prod(factor_image, shrink[:, None] * projected)
            next_coef = -jax.scipy.linalg.solve_triangular(chol_lower, image_new, lower=True)
            direction = scaled + jnp.dot(unit_dir, next_coef, precision=lax.Precision.HIGHEST)
    column_start = lax.axis_index("rhs") * col_share
    out_sol = lax.dynamic_slice_in_dim(solution, column_start, col_share, 1)
    out_res = lax.dynamic_slice_in_dim(residual, column_start, col_share, 1)
    return (out_sol, out_res)


def solution(mesh):
    placed = (P(("samples", "rhs"), "features"), P("features", "rhs"), P("features", "rhs"), P())
    return jax.shard_map(
        shards,
        mesh=mesh,
        in_specs=placed,
        out_specs=(P("features", "rhs"), P("features", "rhs")),
        check_vma=False,
    )
```

profile of v0, /device:TPU:0, one launch (start us, length us, event | category | flops | bytes accessed | tf_op | source)
XLA Modules:
  0.0 853.2 jit_solution(9998928612973178029)
XLA Ops:
  10.0 12.9 %all-gather.3.cloned.1.call-done = f32[8192,64]{0,1:T(8,128)} async-done(((f32[8192,32]{0,1:T(8,128)}), f32[8192,64]{0,1:T(8,128)}) %all-gather.3.cloned.1.call-update) | async-done | bytes 2097168 | tf_op jit(solution)/shard_map/all_gather | solution.py:47
  24.7 25.6 %all-gather.5.cloned.1.call-done = bf16[8192,768]{1,0:T(8,128)(2,1)} async-done(((bf16[8192,384]{1,0:T(8,128)(2,1)}), bf16[8192,768]{1,0:T(8,128)(2,1)}) %all-gather.5.cloned.1.call-update) | async-done | bytes 12582928 | tf_op jit(solution)/shard_map/all_gather | solution.py:49
  61.5 36.2 %all-reduce.15.cloned.1.call-done = f32[768,64]{0,1:T(8,128)} async-done(((f32[768,64]{0,1:T(8,128)}), f32[768,64]{0,1:T(8,128)}) %all-reduce.15.cloned.1.call-update) | async-done | bytes 196624 | tf_op jit(solution)/shard_map/psum | solution.py:52
  98.7 8.5 fusion.67
  107.2 9.8 %fusion.3 = f32[8192,64]{0,1:T(8,128)} fusion(f32[8192,64]{0,1:T(8,128)S(1)} %copy-done.1, f32[64,8192]{1,0:T(8,128)S(1)} %fusion.67, bf16[8192,768]{1,0:T(8,128)(2,1)} %all-gather.5.cloned.1.call-done, bf16[768,64]{0,1:T(8,128)(2,1)S(1)} %multiply_convert_fusion, f32[768,64]{0,1:T(8,128)S(1)} %copy-done.19, f32[768]{0:T(1024)S(1)} %divide_add_fusion), kind=kOutput, calls=%fused_computation.13 | convolution fusion | flops 806551552 | bytes 19172352 | tf_op jit(solution)/shard_map/dot_general | solution.py:40
  117.1 30.4 %convolution_bitcast_fusion.5 = f32[4096,64]{0,1:T(8,128)S(1)} fusion(bf16[4096,8192]{1,0:T(8,128)(2,1)} %param.11, f32[8192,64]{0,1:T(8,128)} %fusion.3), kind=kOutput, calls=%fused_computation.18 | convolution fusion | flops 4295491584 | bytes 70254592 | tf_op jit(solution)/shard_map/dot_general | solution.py:62
  147.4 42.8 %all-reduce.30 = bf16[4096,64]{0,1:T(8,128)(2,1)} all-reduce(f32[4096,64]{0,1:T(8,128)S(1)} %convolution_bitcast_fusion.5), channel_id=1, replica_groups=mesh['samples'=4,'features'=4,'rhs'=2] {'features'}, use_global_device_ids=true, to_apply=%region_2.0 | all-reduce | flops 262144 | bytes 1572864 | tf_op jit(solution)/shard_map/psum | solution.py:63
  190.2 25.9 %convolution_bitcast_fusion.2 = f32[8192,64]{0,1:T(8,128)} fusion(bf16[4096,8192]{1,0:T(8,128)(2,1)} %param.11, bf16[4096,64]{0,1:T(8,128)(2,1)} %all-reduce.30), kind=kOutput, calls=%fused_computation.10 | convolution fusion | flops 4294967296 | bytes 69730304 | tf_op jit(solution)/shard_map/dot_general | solution.py:64
  220.2 57.3 %all-reduce.17.cloned.1.call-done = f32[8192,64]{0,1:T(8,128)} async-done(((f32[8192,64]{0,1:T(8,128)}), f32[8192,64]{0,1:T(8,128)}) %all-reduce.17.cloned.1.call-update) | async-done | bytes 2097168 | tf_op jit(solution)/shard_map/psum | solution.py:67
  302.0 19.4 %all-reduce.29.cloned.1.call-done = (f32[64,64]{1,0:T(8,128)}, f32[64,64]{1,0:T(8,128)}, f32[64,64]{1,0:T(8,128)}, f32[64,64]{1,0:T(8,128)}) async-done(((f32[64,64]{1,0:T(8,128)}, f32[64,64]{1,0:T(8,128)}, f32[64,64]{1,0:T(8,128)}, f32[64,64]{1,0:T(8,128)}), (f32[64,64]{1,0:T(8,128)}, f32[64,64]{1,0:T(8,128)}, f32[64,64]{1,0:T(8,128)}, f32[64,64]{1,0:T(8,128)})) %all-reduce.29.cloned.1.call-update) | async-done | bytes 65552 | tf_op jit(solution)/shard_map/psum | solution.py:52
  344.5 14.6 %all-reduce.19.cloned.1.call-done = f32[768,64]{0,1:T(8,128)} async-done(((f32[768,64]{0,1:T(8,128)}), f32[768,64]{0,1:T(8,128)}) %all-reduce.19.cloned.1.call-update) | async-done | bytes 196624 | tf_op jit(solution)/shard_map/psum | solution.py:52
  370.6 8.6 %fusion.4 = f32[8192,64]{0,1:T(8,128)S(1)} fusion(f32[8192,64]{0,1:T(8,128)S(1)} %convolution_subtract_fusion.1, f32[64,8192]{1,0:T(8,128)S(1)} %fusion.72, bf16[8192,768]{1,0:T(8,128)(2,1)} %all-gather.5.cloned.1.call-done, bf16[768,64]{0,1:T(8,128)(2,1)S(1)} %get-tuple-element.20, f32[768,64]{0,1:T(8,128)S(1)} %get-tuple-element.21, ...), kind=kOutput, calls=%fused_computation.14 | convolution fusion | flops 806551552 | bytes 19172352 | tf_op jit(solution)/shard_map/dot_general | solution.py:40
  381.5 27.8 %convolution_bitcast_fusion.4 = f32[4096,64]{0,1:T(8,128)S(1)} fusion(bf16[4096,8192]{1,0:T(8,128)(2,1)} %param.11, f32[8192,64]{0,1:T(8,128)S(1)} %convolution_add_fusion.2), kind=kOutput, calls=%fused_computation.17 | convolution fusion | flops 4295491584 | bytes 70254592 | tf_op jit(solution)/shard_map/dot_general | solution.py:62
  409.4 42.1 %all-reduce.31 = bf16[4096,64]{0,1:T(8,128)(2,1)} all-reduce(f32[4096,64]{0,1:T(8,128)S(1)} %convolution_bitcast_fusion.4), channel_id=1, replica_groups=mesh['samples'=4,'features'=4,'rhs'=2] {'features'}, use_global_device_ids=true, to_apply=%region_11.0 | all-reduce | flops 262144 | bytes 1572864 | tf_op jit(solution)/shard_map/psum | solution.py:63
  451.5 25.9 %convolution_bitcast_fusion.1 = f32[8192,64]{0,1:T(8,128)} fusion(bf16[4096,8192]{1,0:T(8,128)(2,1)} %param.11, bf16[4096,64]{0,1:T(8,128)(2,1)} %all-reduce.31), kind=kOutput, calls=%fused_computation.5 | convolution fusion | flops 4294967296 | bytes 69730304 | tf_op jit(solution)/shard_map/dot_general | solution.py:64
  481.9 57.4 %all-reduce.21.cloned.1.call-done = f32[8192,64]{0,1:T(8,128)} async-done(((f32[8192,64]{0,1:T(8,128)}), f32[8192,64]{0,1:T(8,128)}) %all-reduce.21.cloned.1.call-update) | async-done | bytes 2097168 | tf_op jit(solution)/shard_map/psum | solution.py:67
  564.2 19.4 %all-reduce.27.cloned.1.call-done = (f32[64,64]{1,0:T(8,128)}, f32[64,64]{1,0:T(8,128)}, f32[64,64]{1,0:T(8,128)}, f32[64,64]{1,0:T(8,128)}) async-done(((f32[64,64]{1,0:T(8,128)}, f32[64,64]{1,0:T(8,128)}, f32[64,64]{1,0:T(8,128)}, f32[64,64]{1,0:T(8,128)}), (f32[64,64]{1,0:T(8,128)}, f32[64,64]{1,0:T(8,128)}, f32[64,64]{1,0:T(8,128)}, f32[64,64]{1,0:T(8,128)})) %all-reduce.27.cloned.1.call-update) | async-done | bytes 65552 | tf_op jit(solution)/shard_map/psum | solution.py:52
  606.6 14.8 %all-reduce.23.cloned.1.call-done = f32[768,64]{0,1:T(8,128)} async-done(((f32[768,64]{0,1:T(8,128)}), f32[768,64]{0,1:T(8,128)}) %all-reduce.23.cloned.1.call-update) | async-done | bytes 196624 | tf_op jit(solution)/shard_map/psum | solution.py:52
  632.9 8.6 %fusion.5 = f32[8192,64]{0,1:T(8,128)S(1)} fusion(f32[8192,64]{0,1:T(8,128)S(1)} %convolution_subtract_fusion, f32[64,8192]{1,0:T(8,128)S(1)} %fusion.79, bf16[8192,768]{1,0:T(8,128)(2,1)} %all-gather.5.cloned.1.call-done, f32[768,64]{0,1:T(8,128)S(1)} %get-tuple-element.23, bf16[768,64]{0,1:T(8,128)(2,1)S(1)} %get-tuple-element.22), kind=kOutput, calls=%fused_computation.15 | convolution fusion | flops 806502400 | bytes 19169280 | tf_op jit(solution)/shard_map/dot_general | solution.py:40
  644.0 27.1 %convolution_bitcast_fusion.3 = f32[4096,64]{0,1:T(8,128)S(1)} fusion(bf16[4096,8192]{1,0:T(8,128)(2,1)} %param.11, f32[8192,64]{0,1:T(8,128)S(1)} %convolution_add_fusion), kind=kOutput, calls=%fused_computation.16 | convolution fusion | flops 4295491584 | bytes 70254592 | tf_op jit(solution)/shard_map/dot_general | solution.py:62
  671.1 42.1 %all-reduce.32 = bf16[4096,64]{0,1:T(8,128)(2,1)} all-reduce(f32[4096,64]{0,1:T(8,128)S(1)} %convolution_bitcast_fusion.3), channel_id=1, replica_groups=mesh['samples'=4,'features'=4,'rhs'=2] {'features'}, use_global_device_ids=true, to_apply=%region_18.0 | all-reduce | flops 262144 | bytes 1572864 | tf_op jit(solution)/shard_map/psum | solution.py:63
  713.2 25.9 %convolution_bitcast_fusion = f32[8192,64]{0,1:T(8,128)} fusion(bf16[4096,8192]{1,0:T(8,128)(2,1)} %param.11, bf16[4096,64]{0,1:T(8,128)(2,1)} %all-reduce.32), kind=kOutput, calls=%fused_computation | convolution fusion | flops 4294967296 | bytes 69730304 | tf_op jit(solution)/shard_map/dot_general | solution.py:64
  750.0 50.6 %all-reduce.25.cloned.1.call-done = f32[8192,64]{0,1:T(8,128)} async-done(((f32[8192,64]{0,1:T(8,128)}), f32[8192,64]{0,1:T(8,128)}) %all-reduce.25.cloned.1.call-update) | async-done | bytes 2097168 | tf_op jit(solution)/shard_map/psum | solution.py:67
  804.1 19.8 %all-reduce = (f32[64,64]{1,0:T(8,128)S(1)}, f32[64,64]{1,0:T(8,128)S(1)}) all-reduce(f32[64,64]{1,0:T(8,128)S(1)} %fusion.19, f32[64,64]{1,0:T(8,128)S(1)} %fusion.83), channel_id=1, replica_groups=mesh['samples'=4,'features'=4,'rhs'=2] {'features'}, use_global_device_ids=true, to_apply=%region_20.25 | all-reduce | flops 8192 | bytes 65536 | tf_op jit(solution)/shard_map/psum | solution.py:52
  (157 shorter events, 183.9 us)
Async XLA Ops:
  7.2 15.7 %all-gather.3.cloned.1.call-start = ((), (), s32[]{:S(2)}) async-start(), calls=%async_computation | async-start | bytes 3145728 | tf_op jit(solution)/shard_map/all_gather | solution.py:47
  7.9 42.4 %all-gather.5.cloned.1.call-start = ((), (), s32[]{:S(2)}) async-start(), calls=%async_computation.1 | async-start | bytes 18874368 | tf_op jit(solution)/shard_map/all_gather | solution.py:49
  8.7 89.1 %all-reduce.15.cloned.1.call-start = ((), (), s32[]{:S(2)}) async-start(), calls=%async_computation.2 | async-start | bytes 393216 | tf_op jit(solution)/shard_map/psum | solution.py:52
  22.8 27.4 %copy-start.1 = (f32[8192,64]{0,1:T(8,128)S(1)}, f32[8192,64]{0,1:T(8,128)}, u32[]{:S(2)}) copy-start(f32[8192,64]{0,1:T(8,128)} %all-gather.3.cloned.1.call-done) | copy-start | bytes 6291460
  50.3 8.2 copy-start
  61.5 216.0 %all-reduce.17.cloned.1.call-start = ((), (), s32[]{:S(2)}) async-start(), calls=%async_computation.3 | async-start | bytes 4194304 | tf_op jit(solution)/shard_map/psum | solution.py:67
  98.7 8.5 copy-start.19
  216.2 105.3 %all-reduce.29.cloned.1.call-start = ((), (), s32[]{:S(2)}) async-start(), calls=%async_computation.9 | async-start | bytes 262144 | tf_op jit(solution)/shard_map/psum | solution.py:52
  287.3 71.8 %all-reduce.19.cloned.1.call-start = ((), (), s32[]{:S(2)}) async-start(), calls=%async_computation.4 | async-start | bytes 393216 | tf_op jit(solution)/shard_map/psum | solution.py:52
  301.8 237.5 %all-reduce.21.cloned.1.call-start = ((), (), s32[]{:S(2)}) async-start(), calls=%async_computation.5 | async-start | bytes 4194304 | tf_op jit(solution)/shard_map/psum | solution.py:67
  342.2 19.4 %copy-start.24 = (f32[64,64]{1,0:T(8,128)S(1)}, f32[64,64]{1,0:T(8,128)}, u32[]{:S(2)}) copy-start(f32[64,64]{1,0:T(8,128)} %get-tuple-element.14) | copy-start | bytes 49156
  342.2 19.4 %copy-start.25 = (f32[64,64]{1,0:T(8,128)S(1)}, f32[64,64]{1,0:T(8,128)}, u32[]{:S(2)}) copy-start(f32[64,64]{1,0:T(8,128)} %get-tuple-element.15) | copy-start | bytes 49156
  344.3 26.2 %copy-start.7 = (f32[8192,64]{0,1:T(8,128)}, f32[8192,64]{0,1:T(8,128)S(1)}, u32[]{:S(2)}) copy-start(f32[8192,64]{0,1:T(8,128)S(1)} %convolution_subtract_fusion.1) | copy-start | bytes 6291460
  370.5 8.7 %copy-start.13 = (f32[64,8192]{1,0:T(8,128)S(1)}, f32[64,8192]{1,0:T(8,128)}, u32[]{:S(2)}) copy-start(f32[64,8192]{1,0:T(8,128)} %fusion.16) | copy-start | bytes 6291460
  381.5 96.4 %copy-start.5 = (f32[8192,64]{0,1:T(8,128)}, f32[8192,64]{0,1:T(8,128)S(1)}, u32[]{:S(2)}) copy-start(f32[8192,64]{0,1:T(8,128)S(1)} %convolution_add_fusion.2) | copy-start | bytes 6291460
  477.5 106.1 %all-reduce.27.cloned.1.call-start = ((), (), s32[]{:S(2)}) async-start(), calls=%async_computation.8 | async-start | bytes 262144 | tf_op jit(solution)/shard_map/psum | solution.py:52
  549.5 72.0 %all-reduce.23.cloned.1.call-start = ((), (), s32[]{:S(2)}) async-start(), calls=%async_computation.6 | async-start | bytes 393216 | tf_op jit(solution)/shard_map/psum | solution.py:52
  564.0 236.7 %all-reduce.25.cloned.1.call-start = ((), (), s32[]{:S(2)}) async-start(), calls=%async_computation.7 | async-start | bytes 4194304 | tf_op jit(solution)/shard_map/psum | solution.py:67
  604.4 19.7 %copy-start.22 = (f32[64,64]{1,0:T(8,128)S(1)}, f32[64,64]{1,0:T(8,128)}, u32[]{:S(2)}) copy-start(f32[64,64]{1,0:T(8,128)} %get-tuple-element.10) | copy-start | bytes 49156
  604.4 19.7 %copy-start.23 = (f32[64,64]{1,0:T(8,128)S(1)}, f32[64,64]{1,0:T(8,128)}, u32[]{:S(2)}) copy-start(f32[64,64]{1,0:T(8,128)} %get-tuple-element.11) | copy-start | bytes 49156
  606.5 26.5 %copy-start.10 = (f32[8192,64]{0,1:T(8,128)}, f32[8192,64]{0,1:T(8,128)S(1)}, u32[]{:S(2)}) copy-start(f32[8192,64]{0,1:T(8,128)S(1)} %convolution_subtract_fusion) | copy-start | bytes 6291460
  632.9 8.6 %copy-start.14 = (f32[64,8192]{1,0:T(8,128)S(1)}, f32[64,8192]{1,0:T(8,128)}, u32[]{:S(2)}) copy-start(f32[64,8192]{1,0:T(8,128)} %fusion.12) | copy-start | bytes 6291460
  739.9 5.0 copy-start.15
  840.4 4.1 copy-start.18
  (15 other events, 31.6 us)
Sparse Core Ops, SparseCore 0:
  9.5 13.2 all-gather.2
  24.4 25.8 all-gather.4
  61.6 36.1 all-reduce.14
  216.3 61.1 all-reduce.16
  287.4 33.9 all-reduce.28
  324.2 34.8 all-reduce.18
  477.6 61.6 all-reduce.20
  549.6 33.9 all-reduce.26
  586.5 34.9 all-reduce.22
  739.3 61.3 all-reduce.24
where the time goes:
time: 862 us; the launch traced here: 853 us
  matrix products  328 us (38%)
  waiting for transfers between devices  310 us (36%)
  blocking collectives  147 us (17%)
  other arithmetic  47.9 us (6%)
  between operations  15.6 us (2%)
    psum x3, waiting for transfers between devices, shards(): summed = lax.psum(feature_term, ('samples', 'rhs'))  165 us
    psum x3, blocking collectives, shards(): lax.psum(apply_partial_value, 'features').astype(jnp.bfloat16)  127 us
    psum x5, waiting for transfers between devices, totals(): return lax.psum(values, 'features')  105 us
    dot_general x3, matrix products, shards(): jnp.dot(design, narrow, preferred_element_type=jnp.float32)  85.3 us
    dot_general x3, matrix products, shards(): lax.dot_general(design, narrow_images, (((0,), (0,)), ((), ())), preferre...  77.8 us
    dot_general x12, matrix products, inner_prod(): lax.dot_general(left, right, (((0,), (0,)), ((), ())), precision=lax.Prec...  30.3 us
    dot_general x3, matrix products, factor_times(): second = jnp.dot(factor_narrow, lower, preferred_element_type=jnp.float32)  27.1 us
    all_gather x1, waiting for transfers between devices, shards(): basis_rows = lax.all_gather(factor, 'rhs', axis=1, tiled=True)  25.6 us
  transfers between devices with their start and end apart: 10, of which 10 were waited for; matrix products, arithmetic and copies ran while one was open for 11% of the time, Pallas kernels for 0%

commit v1 on v0

v1 whole, which is shorter than its diff:
```python
import functools

import jax
import jax.numpy as jnp
from jax import lax
from jax.experimental import pallas as pl
from jax.experimental.pallas import tpu as pltpu
from jax.sharding import PartitionSpec as P

ITERS = 3

ridge_weight = 1.0

bf16 = jnp.bfloat16
f32 = jnp.float32
NT = (((1,), (1,)), ((), ()))
VMEM = pl.BlockSpec(memory_space=pltpu.VMEM)
HBM = pl.BlockSpec(memory_space=pl.ANY)
SMEM = pl.BlockSpec(memory_space=pltpu.SMEM)


def exact(left, right, dims=(((1,), (0,)), ((), ()))):
    return lax.dot_general(left, right, dims, precision=lax.Precision.HIGHEST, preferred_element_type=f32)


def with_narrow(values, narrow, dims):
    upper = values.astype(bf16)
    lower = (values - upper.astype(f32)).astype(bf16)
    first = lax.dot_general(upper, narrow, dims, preferred_element_type=f32)
    return first + lax.dot_general(lower, narrow, dims, preferred_element_type=f32)


def call(body, outs, args, specs, name, scratch=(), flops=0, bytes_accessed=0, limit=None):
    params = pltpu.CompilerParams(vmem_limit_bytes=limit) if limit else pltpu.CompilerParams()
    return pl.pallas_call(
        body,
        name=name,
        out_shape=[jax.ShapeDtypeStruct(shape, dtype) for shape, dtype in outs],
        in_specs=specs,
        out_specs=[VMEM] * len(outs),
        scratch_shapes=list(scratch),
        compiler_params=params,
        cost_estimate=pl.CostEstimate(flops=flops, bytes_accessed=bytes_accessed, transcendentals=0),
    )(*args)


def exchange(values, axis, size, mask):
    return lax.ppermute(values, axis, [(at, at ^ mask) for at in range(size)])


def stream_rows(design_ref, buffers, sems, first_sem, row_of, groups, per, tile, use):
    depth = buffers.shape[0]
    steps = groups * per
    half = tile // 2

    def copy(step):
        slot = lax.rem(step, depth)
        return pltpu.make_async_copy(
            design_ref.at[pl.ds(pl.multiple_of(row_of(step), tile), tile), :], buffers.at[slot], sems.at[slot]
        )

    def copy_half(side):
        return pltpu.make_async_copy(
            design_ref.at[pl.ds(pl.multiple_of(row_of(0) + side * half, half), half), :],
            buffers.at[0, pl.ds(side * half, half), :],
            first_sem.at[side],
        )

    def begin():
        copy_half(0).start()
        copy_half(1).start()
        for step in range(1, min(depth, steps)):
            copy(step).start()

    def run():
        for group in range(groups):
            if group == 0:
                for side in range(2):
                    copy_half(side).wait()
                    use(0, side * half, buffers[0, side * half : (side + 1) * half, :])
                if steps > depth:
                    copy(depth).start()

            def one(j, carry):
                step = group * per + j
                copy(step).wait()
                use(group, pl.multiple_of(j * tile, tile), buffers[lax.rem(step, depth)])

                @pl.when(step + depth < steps)
                def _():
                    copy(step + depth).start()

                return carry

            lax.fori_loop(1 if group == 0 else 0, per, one, 0)

    return begin, run


def place_shares(where, stacks, target, samples, rhs, width, turn):
    for across in range(rhs):
        for mask in range(samples):
            share = (where[2] ^ across) * samples + (where[1] ^ mask)
            start = pl.multiple_of(share * width, width)
            piece = stacks[across][mask]
            if turn:
                target[pl.ds(start, width), :] = jnp.swapaxes(piece.astype(f32), 0, 1).astype(target.dtype)
            else:
                target[:, pl.ds(start, width)] = piece


def forward_pass(where, stacks, design, masks, sizes):
    samples, feats, rhs = sizes
    rows, depth = design.shape
    cols = stacks[0].shape[1]
    chunk = rows // feats
    tile = min(256, chunk)
    per = chunk // tile
    width = depth // (samples * rhs)

    def body(where_ref, design_ref, *refs):
        stack_refs = refs[:rhs]
        outs = refs[rhs : rhs + len(masks)]
        buffers, turned, sems, first_sem = refs[rhs + len(masks) :]
        at = [where_ref[i] for i in range(3)]

        def row_of(step):
            return (at[0] ^ (masks[0] - step // per)) * chunk + lax.rem(step, per) * tile

        def use(group, start, block):
            out = jnp.dot(block, turned[...], preferred_element_type=f32)
            outs[group][:, pl.ds(start, block.shape[0])] = jnp.swapaxes(out, 0, 1).astype(bf16)

        begin, run = stream_rows(design_ref, buffers, sems, first_sem, row_of, len(masks), per, tile, use)
        begin()
        place_shares(at, stack_refs, turned, samples, rhs, width, True)
        run()

    work = len(masks) * chunk * depth
    return call(
        body,
        [((cols, chunk), bf16)] * len(masks),
        (where, design, *stacks),
        [SMEM, HBM] + [VMEM] * rhs,
        "forward",
        scratch=(
            pltpu.VMEM((4, tile, depth), bf16),
            pltpu.VMEM((depth, cols), bf16),
            pltpu.SemaphoreType.DMA((4,)),
            pltpu.SemaphoreType.DMA((2,)),
        ),
        flops=2 * work * cols,
        bytes_accessed=2 * work,
        limit=40 << 20,
    )


def backward_pass(where, pieces, design, masks, sizes, carried=None):
    samples, feats, rhs = sizes
    rows, depth = design.shape
    cols = pieces[0].shape[0]
    chunk = rows // feats
    tile = min(256, chunk)
    per = chunk // tile
    width = depth // (samples * rhs)
    n = len(masks)

    def body(where_ref, design_ref, *refs):
        piece_refs = refs[:n]
        last = carried is not None
        if last:
            start_ref, mine_ref, theirs_ref, buffers, total, sems, first_sem = refs[n:]
        else:
            total, buffers, sems, first_sem = refs[n:]
        at = [where_ref[i] for i in range(3)]

        def row_of(step):
            return (at[0] ^ (masks[0] + step // per)) * chunk + lax.rem(step, per) * tile

        def use(group, start, block):
            left = piece_refs[group][:, pl.ds(start, block.shape[0])]
            out = jnp.dot(left, block, preferred_element_type=f32)
            if group == 0 and isinstance(start, int) and start == 0:
                total[...] = start_ref[...] + out if last else out
            else:
                total[...] += out

        begin, run = stream_rows(design_ref, buffers, sems, first_sem, row_of, n, per, tile, use)
        begin()
        run()
        if last:
            for side, out in ((0, mine_ref), (1, theirs_ref)):
                for mask in range(samples):
                    share = (at[2] ^ side) * samples + (at[1] ^ mask)
                    out[mask] = total[:, pl.ds(pl.multiple_of(share * width, width), width)].astype(bf16)

    work = n * chunk * depth
    buffers = pltpu.VMEM((4, tile, depth), bf16)
    sems = (pltpu.SemaphoreType.DMA((4,)), pltpu.SemaphoreType.DMA((2,)))
    args = (where, design, *pieces)
    specs = [SMEM, HBM] + [VMEM] * n
    if carried is None:
        outs = [((cols, depth), f32)]
        scratch = (buffers, *sems)
    else:
        outs = [((samples, cols, width), bf16)] * 2
        args += (carried,)
        specs += [VMEM]
        scratch = (buffers, pltpu.VMEM((cols, depth), f32), *sems)
    return call(
        body, outs, args, specs, "backward", scratch=scratch, flops=2 * work * cols, bytes_accessed=2 * work, limit=40 << 20
    )


def merge(mine, theirs, samples, rhs, sent_dtype):
    came = exchange(theirs, "rhs", rhs, 1)
    sums = [mine[mask].astype(f32) + came[mask].astype(f32) for mask in range(samples)]
    return [sums[0]] + [one.astype(sent_dtype) for one in sums[1:]]


def sum_small(values, sizes):
    for axis, size in zip(("rhs", "samples", "features"), (sizes[2], sizes[0], sizes[1])):
        mask = 1
        while mask < size:
            values = values + exchange(values, axis, size, mask)
            mask *= 2
    return values


def share_all(values, samples, rhs):
    stack = jnp.stack([values] + [exchange(values, "samples", samples, mask) for mask in range(1, samples)])
    return [stack] + [exchange(stack, "rhs", rhs, mask) for mask in range(1, rhs)]


def sum_all(where, mine, theirs, sizes):
    samples, feats, rhs = sizes
    pieces = merge(mine, theirs, samples, rhs, f32)
    total = pieces[0]
    for mask in range(1, samples):
        total = total + exchange(pieces[mask], "samples", samples, mask)
    whole = total
    for mask in range(1, feats):
        whole = whole + exchange(total, "features", feats, mask)
    return share_all(whole, samples, rhs)


def write_halves(where_ref, packed, mine_ref, theirs_ref):
    samples, cols, width = mine_ref.shape
    for side, out in ((0, mine_ref), (1, theirs_ref)):
        for mask in range(samples):
            share = (where_ref[2] ^ side) * samples + (where_ref[1] ^ mask)
            out[mask] = packed[:, pl.ds(pl.multiple_of(share * width, width), width)]


def first_products(where, res, basis, wide, sizes):
    cols, rank = res.shape[0], basis.shape[1]

    def body(where_ref, res_ref, basis_ref, mine_ref, theirs_ref, packed):
        packed[...] = jnp.zeros_like(packed)
        packed[:, :rank] = with_narrow(res_ref[...], basis_ref[...], (((1,), (0,)), ((), ())))
        write_halves(where_ref, packed, mine_ref, theirs_ref)

    return call(
        body,
        [((sizes[0], cols, wide // (sizes[0] * sizes[2])), f32)] * 2,
        (where, res, basis),
        [SMEM, VMEM, VMEM],
        "first_products",
        scratch=(pltpu.VMEM((cols, wide), f32),),
    )


def first_update(where, stacks, res, basis, shrink, sizes):
    samples, feats, rhs = sizes
    cols, own = res.shape
    rank = basis.shape[1]
    width = stacks[0].shape[2]
    wide = width * samples * rhs

    def body(where_ref, *refs):
        stack_refs = refs[:rhs]
        res_ref, basis_ref, shrink_ref, proj_ref, dir_ref, narrow_ref, packed = refs[rhs:]
        at = [where_ref[i] for i in range(3)]
        place_shares(at, stack_refs, packed, samples, rhs, width, False)
        proj = packed[:, :rank]
        proj_ref[...] = proj
        direction = res_ref[...] + with_narrow(proj * shrink_ref[...], basis_ref[...], NT)
        dir_ref[...] = direction
        narrow_ref[...] = direction.astype(bf16)

    return call(
        body,
        [((cols, rank), f32), ((cols, own), f32), ((cols, own), bf16)],
        (where, *stacks, res, basis, shrink),
        [SMEM] + [VMEM] * (rhs + 3),
        "first_update",
        scratch=(pltpu.VMEM((cols, wide), f32),),
    )


def products(where, kept, arrived, direction, res, basis, wide, sizes):
    cols, own = res.shape
    rank = basis.shape[1]
    n = len(arrived)

    def body(where_ref, kept_ref, *refs):
        arrived_refs = refs[:n]
        dir_ref, res_ref, basis_ref, applied_ref, mine_ref, theirs_ref, packed = refs[n:]
        applied = kept_ref[...]
        for ref in arrived_refs:
            applied = applied + ref[...].astype(f32)
        direction_now, residual = dir_ref[...], res_ref[...]
        applied = applied + ridge_weight * direction_now
        applied_ref[...] = applied
        packed[...] = jnp.zeros_like(packed)
        packed[:, rank : rank + cols] = exact(direction_now, applied, NT)
        packed[:, rank + cols : rank + 2 * cols] = exact(residual, direction_now, NT)
        packed[:, :rank] = with_narrow(applied, basis_ref[...], (((1,), (0,)), ((), ())))
        packed[:, rank + 2 * cols : rank + 3 * cols] = exact(applied, applied, NT)
        packed[:, rank + 3 * cols : rank + 4 * cols] = exact(residual, applied, NT)
        write_halves(where_ref, packed, mine_ref, theirs_ref)

    return call(
        body,
        [((cols, own), f32)] + [((sizes[0], cols, wide // (sizes[0] * sizes[2])), f32)] * 2,
        (where, kept, *arrived, direction, res, basis),
        [SMEM] + [VMEM] * (n + 4),
        "products",
        scratch=(pltpu.VMEM((cols, wide), f32),),
    )


def inverse(matrix):
    size = matrix.shape[0]
    row_at = lax.broadcasted_iota(jnp.int32, (size, 1), 0)
    unit = lax.broadcasted_iota(jnp.int32, (size, size), 0) == lax.broadcasted_iota(jnp.int32, (size, size), 1)
    work = jnp.concatenate([matrix, unit.astype(f32)], axis=1)
    for k in range(size):
        row = work[k : k + 1, :]
        recip = 1.0 / row[:, k : k + 1]
        column = work[:, k : k + 1]
        scale = jnp.where(row_at == k, 1.0 - recip, column * recip)
        work = work - scale * row
    return work[:, size:]


def update(where, stacks, proj, direction, applied, res, basis, shrink, sizes):
    samples, feats, rhs = sizes
    cols, own = res.shape
    rank = basis.shape[1]
    width = stacks[0].shape[2]
    wide = width * samples * rhs

    def body(where_ref, *refs):
        stack_refs = refs[:rhs]
        proj_ref, dir_ref, applied_ref, res_ref, basis_ref, shrink_ref, step_ref, new_res_ref = refs[rhs : rhs + 8]
        packed = refs[-1]
        at = [where_ref[i] for i in range(3)]
        place_shares(at, stack_refs, packed, samples, rhs, width, False)
        gram = packed[:, rank : rank + cols]
        gram = 0.5 * (gram + jnp.swapaxes(gram, 0, 1))
        inv = inverse(gram)
        inv = 0.5 * (inv + jnp.swapaxes(inv, 0, 1))
        step = exact(packed[:, rank + cols : rank + 2 * cols], inv)
        step_ref[...] = step
        residual = res_ref[...] - exact(step, applied_ref[...])
        new_res_ref[...] = residual
        new_proj_ref, new_dir_ref, narrow_ref = refs[rhs + 8 : -1]
        image = packed[:, :rank]
        new_proj = proj_ref[...] - exact(step, image)
        new_proj_ref[...] = new_proj
        scaled = new_proj * shrink_ref[...]
        cross = packed[:, rank + 3 * cols : rank + 4 * cols] - exact(step, packed[:, rank + 2 * cols : rank + 3 * cols])
        cross = cross + exact(scaled, image, NT)
        next_coef = -exact(cross, inv)
        new_dir = residual + with_narrow(scaled, basis_ref[...], NT) + exact(next_coef, dir_ref[...])
        new_dir_ref[...] = new_dir
        narrow_ref[...] = new_dir.astype(bf16)

    outs = [((cols, cols), f32), ((cols, own), f32)]
    outs += [((cols, rank), f32), ((cols, own), f32), ((cols, own), bf16)]
    return call(
        body,
        outs,
        (where, *stacks, proj, direction, applied, res, basis, shrink),
        [SMEM] + [VMEM] * (rhs + 6),
        "update",
        scratch=(pltpu.VMEM((cols, wide), f32),),
    )


def gram_part(kept, came, direction, res):
    cols, chunk = kept.shape
    n = len(came)

    def body(kept_ref, *refs):
        dir_ref, res_ref, image_ref, gram_ref = refs[n:]
        total = kept_ref[...].astype(f32)
        for ref in refs[:n]:
            total = total + ref[...].astype(f32)
        image = total.astype(bf16)
        image_ref[...] = image
        direction_now = dir_ref[...]
        gram = exact(total, image.astype(f32), NT) + ridge_weight * exact(direction_now, direction_now, NT)
        gram_ref[:, :cols] = gram
        gram_ref[:, cols:] = exact(res_ref[...], direction_now, NT)

    return call(
        body, [((cols, chunk), bf16), ((cols, 2 * cols), f32)], (kept, *came, direction, res), [VMEM] * (n + 3), "gram_part"
    )


def last_step(grams):
    cols = grams.shape[0]

    def body(gram_ref, step_ref):
        gram = gram_ref[:, :cols]
        inv = inverse(0.5 * (gram + jnp.swapaxes(gram, 0, 1)))
        step_ref[...] = exact(gram_ref[:, cols:], 0.5 * (inv + jnp.swapaxes(inv, 0, 1)))

    return call(body, [((cols, cols), f32)], (grams,), [VMEM], "last_step")[0]


def last_residual(where, kept, arrived, direction, res, step, part):
    cols, own = res.shape
    n = len(arrived)

    def body(where_ref, kept_ref, *refs):
        dir_ref, res_ref, step_ref, same_ref, other_ref, whole = refs[n:]
        applied = kept_ref[...]
        for ref in refs[:n]:
            applied = applied + ref[...].astype(f32)
        applied = applied + ridge_weight * dir_ref[...]
        whole[...] = res_ref[...] - exact(step_ref[...], applied)
        same_ref[...] = whole[pl.ds(pl.multiple_of(where_ref[2] * part, part), part), :].astype(bf16)
        other_ref[...] = whole[pl.ds(pl.multiple_of((where_ref[2] ^ 1) * part, part), part), :].astype(bf16)

    return call(
        body,
        [((part, own), bf16)] * 2,
        (where, kept, *arrived, direction, res, step),
        [SMEM] + [VMEM] * (n + 4),
        "last_residual",
        scratch=(pltpu.VMEM((cols, own), f32),),
    )


def collect(where, all_stacks, steps, sizes):
    samples, feats, rhs = sizes
    cols, width = all_stacks[0][0].shape[1:]
    part = cols // rhs
    count = len(all_stacks)
    depth = width * samples * rhs

    def body(where_ref, *refs):
        stack_refs, step_refs, out_ref = refs[: count * rhs], refs[count * rhs : -1], refs[-1]
        at = [where_ref[i] for i in range(3)]
        rows = pl.ds(pl.multiple_of(at[2] * part, part), part)
        coefs = [ref[rows, :] for ref in step_refs]
        for across in range(rhs):
            for mask in range(samples):
                share = (at[2] ^ across) * samples + (at[1] ^ mask)
                total = jnp.zeros((part, width), f32)
                for k in range(count):
                    upper = coefs[k].astype(bf16)
                    lower = (coefs[k] - upper.astype(f32)).astype(bf16)
                    block = stack_refs[k * rhs + across][mask]
                    total += jnp.dot(upper, block, preferred_element_type=f32)
                    total += jnp.dot(lower, block, preferred_element_type=f32)
                out_ref[:, pl.ds(pl.multiple_of(share * width, width), width)] = total

    return call(
        body,
        [((part, depth), f32)],
        (where, *[one for stacks in all_stacks for one in stacks], *steps),
        [SMEM] + [VMEM] * (count * rhs + count),
        "collect",
    )[0]


def shards(sizes, design, right_side, factor, nystrom_values):
    samples, feats, rhs = sizes
    depth, col_share = right_side.shape
    own = depth // (samples * rhs)
    at_sample, at_feat, at_rhs = lax.axis_index("samples"), lax.axis_index("features"), lax.axis_index("rhs")
    where = jnp.stack([at_feat, at_sample, at_rhs]).astype(jnp.int32)
    shrink = ((1.0 + jnp.min(nystrom_values)) / (1.0 + nystrom_values) - 1.0)[None, :]
    rank = shrink.shape[1]
    cols = col_share * rhs
    unit = 128 * samples * rhs
    wide = -(-(rank + 4 * cols) // unit) * unit

    def own_rows(block):
        mine = lax.dynamic_slice_in_dim(block, (at_rhs * samples + at_sample) * own, own, 0)
        theirs = lax.dynamic_slice_in_dim(block, ((1 - at_rhs) * samples + at_sample) * own, own, 0)
        came = exchange(theirs, "rhs", rhs, 1)
        return jnp.where(at_rhs == 0, jnp.concatenate([mine, came], 1), jnp.concatenate([came, mine], 1))

    res = own_rows(right_side).T
    basis = own_rows(factor)
    proj_stacks = sum_all(where, *first_products(where, res, basis, wide, sizes), sizes)
    proj, direction, narrow = first_update(where, proj_stacks, res, basis, shrink, sizes)
    all_stacks, steps = [], []
    for iteration in range(ITERS):
        last = iteration + 1 == ITERS
        stacks = share_all(narrow, samples, rhs)
        all_stacks.append(stacks)
        away = list(range(feats - 1, 0, -1))
        sent = forward_pass(where, stacks, design, away, sizes)
        came = [exchange(value, "features", feats, mask) for value, mask in zip(sent, away)]
        (kept,) = forward_pass(where, stacks, design, [0], sizes)
        if last:
            image, grams = gram_part(kept, came, direction, res)
            grams = sum_small(grams, sizes)
        else:
            total = kept.astype(f32)
            for value in came:
                total = total + value.astype(f32)
            image = total.astype(bf16)
        others = [exchange(image, "features", feats, mask) for mask in range(1, feats)]
        (carried,) = backward_pass(where, [image], design, [0], sizes)
        mine, theirs = backward_pass(where, others, design, list(range(1, feats)), sizes, carried)
        pieces = merge(mine, theirs, samples, rhs, bf16)
        arrived = [exchange(pieces[mask], "samples", samples, mask) for mask in range(1, samples)]
        if last:
            step = last_step(grams)
            same, other = last_residual(where, pieces[0], arrived, direction, res, step, col_share)
        else:
            applied, *halves = products(where, pieces[0], arrived, direction, res, basis, wide, sizes)
            sums = sum_all(where, *halves, sizes)
            step, res, proj, direction, narrow = update(
                where, sums, proj, direction, applied, res, basis, shrink, sizes
            )
        steps.append(step)
    pair = jnp.stack([same, exchange(other, "rhs", rhs, 1)])
    parts = jnp.stack([pair] + [exchange(pair, "samples", samples, mask) for mask in range(1, samples)])
    out_sol = collect(where, all_stacks, steps, sizes).T
    order = jnp.arange(samples) ^ at_sample
    sides = jnp.arange(rhs) ^ at_rhs
    parts = parts[order][:, sides]
    out_res = parts.transpose(1, 0, 3, 2).reshape(depth, col_share).astype(f32)
    return (out_sol, out_res)


def solution(mesh):
    sizes = (mesh.shape["samples"], mesh.shape["features"], mesh.shape["rhs"])
    placed = (P(("samples", "rhs"), "features"), P("features", "rhs"), P("features", "rhs"), P())
    return jax.shard_map(
        functools.partial(shards, sizes),
        mesh=mesh,
        in_specs=placed,
        out_specs=(P("features", "rhs"), P("features", "rhs")),
        check_vma=False,
    )
```

time: 862 us -> 436 us (0.51)
  matrix products: 328 us -> 0 us
  waiting for transfers between devices: 310 us -> 98.4 us
  Pallas kernels: 0 us -> 209 us
  blocking collectives: 147 us -> 0 us
  starting transfers between devices: 1.16 us -> 92.2 us
  other arithmetic: 47.9 us -> 15.7 us
  between operations: 15.6 us -> 2.38 us
  local copies, waits for them, and re-layouts: 4.31 us -> 13.1 us
    dot_general x42 -> x0, matrix products: 309 us -> none  [the longest x3 85.3 us: shards(): jnp.dot(design, narrow, preferred_element_type=jnp.float32)]
    psum x8 -> x0, waiting for transfers between devices: 270 us -> none  [the longest x3 165 us: shards(): summed = lax.psum(feature_term, ('samples', 'rhs'))]
    pallas_call x0 -> x22, Pallas kernels: none -> 209 us  [call(): pl.pallas_call(body, name=name, out_shape=[jax.ShapeDtypeStruct(shape, dt...]
    psum x4 -> x0, blocking collectives: 147 us -> none  [the longest x3 127 us: shards(): lax.psum(apply_partial_value, 'features').astype(jnp.bfloat16)]
    ppermute x0 -> x86, waiting for transfers between devices: none -> 98.4 us  [exchange(): return lax.ppermute(values, axis, [(at, at ^ mask) for at in range(size)])]
    ppermute x0 -> x86, starting transfers between devices: none -> 92.2 us  [exchange(): return lax.ppermute(values, axis, [(at, at ^ mask) for at in range(size)])]
    all_gather x2 -> x0, waiting for transfers between devices: 38.5 us -> none  [the longest x1 25.6 us: shards(): basis_rows = lax.all_gather(factor, 'rhs', axis=1, tiled=True)]
    another operation x15 -> x9, other arithmetic: 36.2 us -> 4.54 us  [the longest x6 2.94 us: share_all(): jnp.stack([values] + [exchange(values, 'samples', samples, mask) for mask...]
  transfers between devices with their start and end apart: 10 -> 86, of which waited for: 10 -> 55; matrix products, arithmetic and copies ran while one was open for 11% -> 1% of each run, Pallas kernels for 0% -> 14%
where the time goes in v1:
time: 436 us; the launch traced here: 431 us
  Pallas kernels  209 us (48%)
  waiting for transfers between devices  98.4 us (23%)
  starting transfers between devices  92.2 us (21%)
  other arithmetic  15.7 us (4%)
  local copies, waits for them, and re-layouts  13.1 us (3%)
    pallas_call x22, Pallas kernels, call(): pl.pallas_call(body, name=name, out_shape=[jax.ShapeDtypeStruct(shape, dt...  209 us
    ppermute x86, waiting for transfers between devices, exchange(): return lax.ppermute(values, axis, [(at, at ^ mask) for at in range(size)])  98.4 us
    ppermute x86, starting transfers between devices, exchange(): return lax.ppermute(values, axis, [(at, at ^ mask) for at in range(size)])  92.2 us
  transfers between devices with their start and end apart: 86, of which 55 were waited for; matrix products, arithmetic and copies ran while one was open for 1% of the time, Pallas kernels for 14%

profile of v1, /device:TPU:0, one launch (start us, length us, event | category | flops | bytes accessed | tf_op | source)
XLA Modules:
  0.0 430.6 jit_solution(16028936036457338112)
XLA Ops:
  50.0 3.6 collective-permute-done.14
  56.6 18.7 %forward.7 = (bf16[64,1024]{1,0:T(8,128)(2,1)S(1)}, bf16[64,1024]{1,0:T(8,128)(2,1)S(1)}, bf16[64,1024]{1,0:T(8,128)(2,1)S(1)}) custom-call(s32[3]{0:T(128)S(1)} %copy-done.7, bf16[4096,8192]{1,0:T(8,128)(2,1)} %design_ref.23, bf16[4,64,1024]{2,1,0:T(8,128)(2,1)S(1)} %pad_maximum_fusion.refs_0_, bf16[4,64,1024]{2,1,0:T(8,128)(2,1)S(1)} %collective-permute-done.16.refs_1_), custom_call_target="tpu_custom_call" | custom-call | flops 3221225472 | bytes 50331648 | tf_op jit(solution)/shard_map/forward/pallas_call | solution.py:35
  75.7 4.0 collective-permute-start.19
  79.8 8.5 %forward.6 = bf16[64,1024]{1,0:T(8,128)(2,1)S(1)} custom-call(s32[3]{0:T(128)S(1)} %copy-done.7, bf16[4096,8192]{1,0:T(8,128)(2,1)} %design_ref.23, bf16[4,64,1024]{2,1,0:T(8,128)(2,1)S(1)} %pad_maximum_fusion.refs_0_, bf16[4,64,1024]{2,1,0:T(8,128)(2,1)S(1)} %collective-permute-done.16.refs_1_), custom_call_target="tpu_custom_call" | custom-call | flops 1073741824 | bytes 16777216 | tf_op jit(solution)/shard_map/forward/pallas_call | solution.py:35
  92.8 7.3 %backward.6.refs_3_ = f32[64,8192]{1,0:T(8,128)S(1)} custom-call(s32[3]{0:T(128)S(1)} %copy-done.7, bf16[4096,8192]{1,0:T(8,128)(2,1)} %design_ref.23, bf16[64,1024]{1,0:T(8,128)(2,1)S(1)} %add_convert_fusion.10.refs_0_), custom_call_target="tpu_custom_call" | custom-call | flops 1073741824 | bytes 16777216 | tf_op jit(solution)/shard_map/backward/pallas_call | solution.py:35
  101.1 17.6 %backward.7 = (bf16[4,64,1024]{2,1,0:T(8,128)(2,1)S(1)}, bf16[4,64,1024]{2,1,0:T(8,128)(2,1)S(1)}) custom-call(s32[3]{0:T(128)S(1)} %copy-done.7, bf16[4096,8192]{1,0:T(8,128)(2,1)} %design_ref.23, bf16[64,1024]{1,0:T(8,128)(2,1)S(1)} %collective-permute-done.20.refs_0_, bf16[64,1024]{1,0:T(8,128)(2,1)S(1)} %collective-permute-done.21.refs_1_, ...), custom_call_target="tpu_custom_call" | custom-call | flops 3221225472 | bytes 50331648 | tf_op jit(solution)/shard_map/backward/pallas_call | solution.py:35
  130.9 4.2 products.2
  162.3 10.8 %update.2 = (f32[64,64]{1,0:T(8,128)}, f32[64,1024]{1,0:T(8,128)}, f32[64,768]{1,0:T(8,128)}, f32[64,1024]{1,0:T(8,128)}, bf16[64,1024]{1,0:T(8,128)(2,1)}) custom-call(s32[3]{0:T(128)} %pad_add_fusion.where_ref, f32[4,64,128]{2,1,0:T(8,128)} %copy-done.12, f32[4,64,128]{2,1,0:T(8,128)} %copy-done.24, f32[64,768]{1,0:T(8,128)} %get-tuple-element.52.refs_2_, ...), custom_call_target="tpu_custom_call" | custom-call | tf_op jit(solution)/shard_map/update/pallas_call | solution.py:35
  179.3 3.6 collective-permute-done.39
  185.9 18.9 %forward.9 = (bf16[64,1024]{1,0:T(8,128)(2,1)S(1)}, bf16[64,1024]{1,0:T(8,128)(2,1)S(1)}, bf16[64,1024]{1,0:T(8,128)(2,1)S(1)}) custom-call(s32[3]{0:T(128)S(1)} %copy-done.8, bf16[4096,8192]{1,0:T(8,128)(2,1)} %design_ref.23, bf16[4,64,1024]{2,1,0:T(8,128)(2,1)S(1)} %pad_maximum_fusion.1.refs_0_.refs_2_, ...), custom_call_target="tpu_custom_call" | custom-call | flops 3221225472 | bytes 50331648 | tf_op jit(solution)/shard_map/forward/pallas_call | solution.py:35
  209.2 8.5 %forward.8 = bf16[64,1024]{1,0:T(8,128)(2,1)S(1)} custom-call(s32[3]{0:T(128)S(1)} %copy-done.8, bf16[4096,8192]{1,0:T(8,128)(2,1)} %design_ref.23, bf16[4,64,1024]{2,1,0:T(8,128)(2,1)S(1)} %pad_maximum_fusion.1.refs_0_.refs_2_, bf16[4,64,1024]{2,1,0:T(8,128)(2,1)S(1)} %collective-permute-done.41.refs_1_.refs_3_), custom_call_target="tpu_custom_call" | custom-call | flops 1073741824 | bytes 16777216 | tf_op jit(solution)/shard_map/forward/pallas_call | solution.py:35
  223.0 7.3 %backward.8.refs_3_ = f32[64,8192]{1,0:T(8,128)S(1)} custom-call(s32[3]{0:T(128)S(1)} %copy-done.8, bf16[4096,8192]{1,0:T(8,128)(2,1)} %design_ref.23, bf16[64,1024]{1,0:T(8,128)(2,1)S(1)} %add_convert_fusion.6.refs_0_), custom_call_target="tpu_custom_call" | custom-call | flops 1073741824 | bytes 16777216 | tf_op jit(solution)/shard_map/backward/pallas_call | solution.py:35
  231.4 17.4 %backward.9 = (bf16[4,64,1024]{2,1,0:T(8,128)(2,1)S(1)}, bf16[4,64,1024]{2,1,0:T(8,128)(2,1)S(1)}) custom-call(s32[3]{0:T(128)S(1)} %copy-done.8, bf16[4096,8192]{1,0:T(8,128)(2,1)} %design_ref.23, bf16[64,1024]{1,0:T(8,128)(2,1)S(1)} %collective-permute-done.45.refs_0_, bf16[64,1024]{1,0:T(8,128)(2,1)S(1)} %collective-permute-done.46.refs_1_, ...), custom_call_target="tpu_custom_call" | custom-call | flops 3221225472 | bytes 50331648 | tf_op jit(solution)/shard_map/backward/pallas_call | solution.py:35
  261.0 4.2 products.3
  292.9 10.9 %update.3 = (f32[64,64]{1,0:T(8,128)}, f32[64,1024]{1,0:T(8,128)}, f32[64,768]{1,0:T(8,128)}, f32[64,1024]{1,0:T(8,128)}, bf16[64,1024]{1,0:T(8,128)(2,1)}) custom-call(s32[3]{0:T(128)} %pad_add_fusion.where_ref, f32[4,64,128]{2,1,0:T(8,128)} %copy-done.11, f32[4,64,128]{2,1,0:T(8,128)} %copy-done.23, f32[64,768]{1,0:T(8,128)} %get-tuple-element.64.refs_2_, ...), custom_call_target="tpu_custom_call" | custom-call | tf_op jit(solution)/shard_map/update/pallas_call | solution.py:35
  309.9 3.6 collective-permute-done.64
  316.6 19.0 %forward.11 = (bf16[64,1024]{1,0:T(8,128)(2,1)S(1)}, bf16[64,1024]{1,0:T(8,128)(2,1)S(1)}, bf16[64,1024]{1,0:T(8,128)(2,1)S(1)}) custom-call(s32[3]{0:T(128)S(1)} %copy-done.9, bf16[4096,8192]{1,0:T(8,128)(2,1)} %design_ref.23, bf16[4,64,1024]{2,1,0:T(8,128)(2,1)S(1)} %pad_maximum_fusion.2.refs_0_.refs_4_, ...), custom_call_target="tpu_custom_call" | custom-call | flops 3221225472 | bytes 50331648 | tf_op jit(solution)/shard_map/forward/pallas_call | solution.py:35
  340.0 8.5 %forward.10.kept_ref = bf16[64,1024]{1,0:T(8,128)(2,1)S(1)} custom-call(s32[3]{0:T(128)S(1)} %copy-done.9, bf16[4096,8192]{1,0:T(8,128)(2,1)} %design_ref.23, bf16[4,64,1024]{2,1,0:T(8,128)(2,1)S(1)} %pad_maximum_fusion.2.refs_0_.refs_4_, bf16[4,64,1024]{2,1,0:T(8,128)(2,1)S(1)} %collective-permute-done.66.refs_1_.refs_5_), custom_call_target="tpu_custom_call" | custom-call | flops 1073741824 | bytes 16777216 | tf_op jit(solution)/shard_map/forward/pallas_call | solution.py:35
  358.0 7.3 %backward.10.refs_3_ = f32[64,8192]{1,0:T(8,128)S(1)} custom-call(s32[3]{0:T(128)S(1)} %copy-done.9, bf16[4096,8192]{1,0:T(8,128)(2,1)} %design_ref.23, bf16[64,1024]{1,0:T(8,128)(2,1)S(1)} %copy-done.10), custom_call_target="tpu_custom_call" | custom-call | flops 1073741824 | bytes 16777216 | tf_op jit(solution)/shard_map/backward/pallas_call | solution.py:35
  365.7 17.5 %backward.11 = (bf16[4,64,1024]{2,1,0:T(8,128)(2,1)S(1)}, bf16[4,64,1024]{2,1,0:T(8,128)(2,1)S(1)}) custom-call(s32[3]{0:T(128)S(1)} %copy-done.9, bf16[4096,8192]{1,0:T(8,128)(2,1)} %design_ref.23, bf16[64,1024]{1,0:T(8,128)(2,1)S(1)} %collective-permute-done.75.refs_0_, bf16[64,1024]{1,0:T(8,128)(2,1)S(1)} %collective-permute-done.76.refs_1_, ...), custom_call_target="tpu_custom_call" | custom-call | flops 3221225472 | bytes 50331648 | tf_op jit(solution)/shard_map/backward/pallas_call | solution.py:35
  389.6 3.4 collective-permute-done.72
  399.9 4.5 %collective-permute-done.74 = f32[64,128]{1,0:T(8,128)S(1)} collective-permute-done((f32[64,128]{1,0:T(8,128)S(1)}, f32[64,128]{1,0:T(8,128)S(1)}, u32[]{:S(2)}, u32[]{:S(2)}) %collective-permute-start.74) | collective-permute-done | bytes 32800 | tf_op jit(solution)/shard_map/ppermute | solution.py:48
  405.0 7.2 %last_step.1.refs_8_.refs_5_ = f32[64,64]{1,0:T(8,128)} custom-call(f32[64,128]{1,0:T(8,128)} %add.321.gram_ref), custom_call_target="tpu_custom_call" | custom-call | tf_op jit(solution)/shard_map/last_step/pallas_call | solution.py:35
  421.3 3.8 collect.1
  (276 shorter events, 208.0 us)
Async XLA Ops:
  45.3 8.3 %collective-permute-start.14 = (bf16[64,1024]{1,0:T(8,128)(2,1)}, bf16[64,1024]{1,0:T(8,128)(2,1)S(1)}, u32[]{:S(2)}, u32[]{:S(2)}) collective-permute-start(bf16[64,1024]{1,0:T(8,128)(2,1)} %get-tuple-element.43), channel_id=1, source_target_pairs={{0,16},{8,24},{16,0},{24,8},{1,17},{9,25},{17,1},{25,9},{2,18},{10... | collective-permute-start | bytes 393224 | tf_op jit(solution)/shard_map/ppermute | solution.py:48
  75.3 12.9 %collective-permute-start.17 = (bf16[64,1024]{1,0:T(8,128)(2,1)S(1)}, bf16[64,1024]{1,0:T(8,128)(2,1)S(1)}, u32[]{:S(2)}, u32[]{:S(2)}) collective-permute-start(bf16[64,1024]{1,0:T(8,128)(2,1)S(1)} %get-tuple-element.44), channel_id=1, source_target_pairs={{0,6},{2,4},{4,2},{6,0},{1,7},{3,5},{5,3},{7,1},{8,14},{10,12},{12... | collective-permute-start | bytes 393224 | tf_op jit(solution)/shard_map/ppermute | solution.py:48
  75.7 12.5 %collective-permute-start.18 = (bf16[64,1024]{1,0:T(8,128)(2,1)S(1)}, bf16[64,1024]{1,0:T(8,128)(2,1)S(1)}, u32[]{:S(2)}, u32[]{:S(2)}) collective-permute-start(bf16[64,1024]{1,0:T(8,128)(2,1)S(1)} %get-tuple-element.45), channel_id=1, source_target_pairs={{0,4},{2,6},{4,0},{6,2},{1,5},{3,7},{5,1},{7,3},{8,12},{10,14},{12... | collective-permute-start | bytes 393224 | tf_op jit(solution)/shard_map/ppermute | solution.py:48
  75.7 12.5 %collective-permute-start.19 = (bf16[64,1024]{1,0:T(8,128)(2,1)S(1)}, bf16[64,1024]{1,0:T(8,128)(2,1)S(1)}, u32[]{:S(2)}, u32[]{:S(2)}) collective-permute-start(bf16[64,1024]{1,0:T(8,128)(2,1)S(1)} %get-tuple-element.46), channel_id=1, source_target_pairs={{0,2},{2,0},{4,6},{6,4},{1,3},{3,1},{5,7},{7,5},{8,10},{10,8},{12,... | collective-permute-start | bytes 393224 | tf_op jit(solution)/shard_map/ppermute | solution.py:48
  88.4 11.8 %collective-permute-start.20 = (bf16[64,1024]{1,0:T(8,128)(2,1)S(1)}, bf16[64,1024]{1,0:T(8,128)(2,1)S(1)}, u32[]{:S(2)}, u32[]{:S(2)}) collective-permute-start(bf16[64,1024]{1,0:T(8,128)(2,1)S(1)} %add_convert_fusion.10.refs_0_), channel_id=1, source_target_pairs={{0,2},{2,0},{4,6},{6,4},{1,3},{3,1},{5,7},{7,5},{8,10},{10,8},{12,... | collective-permute-start | bytes 393224 | tf_op jit(solution)/shard_map/ppermute | solution.py:48
  88.4 12.7 %collective-permute-start.21 = (bf16[64,1024]{1,0:T(8,128)(2,1)S(1)}, bf16[64,1024]{1,0:T(8,128)(2,1)S(1)}, u32[]{:S(2)}, u32[]{:S(2)}) collective-permute-start(bf16[64,1024]{1,0:T(8,128)(2,1)S(1)} %add_convert_fusion.10.refs_0_), channel_id=1, source_target_pairs={{0,4},{2,6},{4,0},{6,2},{1,5},{3,7},{5,1},{7,3},{8,12},{10,14},{12... | collective-permute-start | bytes 393224 | tf_op jit(solution)/shard_map/ppermute | solution.py:48
  90.0 11.1 %collective-permute-start.22 = (bf16[64,1024]{1,0:T(8,128)(2,1)S(1)}, bf16[64,1024]{1,0:T(8,128)(2,1)S(1)}, u32[]{:S(2)}, u32[]{:S(2)}) collective-permute-start(bf16[64,1024]{1,0:T(8,128)(2,1)S(1)} %add_convert_fusion.10.refs_0_), channel_id=1, source_target_pairs={{0,6},{2,4},{4,2},{6,0},{1,7},{3,5},{5,3},{7,1},{8,14},{10,12},{12... | collective-permute-start | bytes 393224 | tf_op jit(solution)/shard_map/ppermute | solution.py:48
  204.8 12.9 %collective-permute-start.42 = (bf16[64,1024]{1,0:T(8,128)(2,1)S(1)}, bf16[64,1024]{1,0:T(8,128)(2,1)S(1)}, u32[]{:S(2)}, u32[]{:S(2)}) collective-permute-start(bf16[64,1024]{1,0:T(8,128)(2,1)S(1)} %get-tuple-element.55), channel_id=1, source_target_pairs={{0,6},{2,4},{4,2},{6,0},{1,7},{3,5},{5,3},{7,1},{8,14},{10,12},{12... | collective-permute-start | bytes 393224 | tf_op jit(solution)/shard_map/ppermute | solution.py:48
  206.9 11.5 %collective-permute-start.43 = (bf16[64,1024]{1,0:T(8,128)(2,1)S(1)}, bf16[64,1024]{1,0:T(8,128)(2,1)S(1)}, u32[]{:S(2)}, u32[]{:S(2)}) collective-permute-start(bf16[64,1024]{1,0:T(8,128)(2,1)S(1)} %get-tuple-element.56), channel_id=1, source_target_pairs={{0,4},{2,6},{4,0},{6,2},{1,5},{3,7},{5,1},{7,3},{8,12},{10,14},{12... | collective-permute-start | bytes 393224 | tf_op jit(solution)/shard_map/ppermute | solution.py:48
  206.9 11.5 %collective-permute-start.44 = (bf16[64,1024]{1,0:T(8,128)(2,1)S(1)}, bf16[64,1024]{1,0:T(8,128)(2,1)S(1)}, u32[]{:S(2)}, u32[]{:S(2)}) collective-permute-start(bf16[64,1024]{1,0:T(8,128)(2,1)S(1)} %get-tuple-element.57), channel_id=1, source_target_pairs={{0,2},{2,0},{4,6},{6,4},{1,3},{3,1},{5,7},{7,5},{8,10},{10,8},{12,... | collective-permute-start | bytes 393224 | tf_op jit(solution)/shard_map/ppermute | solution.py:48
  218.5 11.8 %collective-permute-start.45 = (bf16[64,1024]{1,0:T(8,128)(2,1)S(1)}, bf16[64,1024]{1,0:T(8,128)(2,1)S(1)}, u32[]{:S(2)}, u32[]{:S(2)}) collective-permute-start(bf16[64,1024]{1,0:T(8,128)(2,1)S(1)} %add_convert_fusion.6.refs_0_), channel_id=1, source_target_pairs={{0,2},{2,0},{4,6},{6,4},{1,3},{3,1},{5,7},{7,5},{8,10},{10,8},{12,... | collective-permute-start | bytes 393224 | tf_op jit(solution)/shard_map/ppermute | solution.py:48
  218.6 12.8 %collective-permute-start.46 = (bf16[64,1024]{1,0:T(8,128)(2,1)S(1)}, bf16[64,1024]{1,0:T(8,128)(2,1)S(1)}, u32[]{:S(2)}, u32[]{:S(2)}) collective-permute-start(bf16[64,1024]{1,0:T(8,128)(2,1)S(1)} %add_convert_fusion.6.refs_0_), channel_id=1, source_target_pairs={{0,4},{2,6},{4,0},{6,2},{1,5},{3,7},{5,1},{7,3},{8,12},{10,14},{12... | collective-permute-start | bytes 393224 | tf_op jit(solution)/shard_map/ppermute | solution.py:48
  221.2 10.2 %collective-permute-start.47 = (bf16[64,1024]{1,0:T(8,128)(2,1)S(1)}, bf16[64,1024]{1,0:T(8,128)(2,1)S(1)}, u32[]{:S(2)}, u32[]{:S(2)}) collective-permute-start(bf16[64,1024]{1,0:T(8,128)(2,1)S(1)} %add_convert_fusion.6.refs_0_), channel_id=1, source_target_pairs={{0,6},{2,4},{4,2},{6,0},{1,7},{3,5},{5,3},{7,1},{8,14},{10,12},{12... | collective-permute-start | bytes 393224 | tf_op jit(solution)/shard_map/ppermute | solution.py:48
  305.3 8.3 %collective-permute-start.64 = (bf16[64,1024]{1,0:T(8,128)(2,1)}, bf16[64,1024]{1,0:T(8,128)(2,1)S(1)}, u32[]{:S(2)}, u32[]{:S(2)}) collective-permute-start(bf16[64,1024]{1,0:T(8,128)(2,1)} %get-tuple-element.66), channel_id=1, source_target_pairs={{0,16},{8,24},{16,0},{24,8},{1,17},{9,25},{17,1},{25,9},{2,18},{10... | collective-permute-start | bytes 393224 | tf_op jit(solution)/shard_map/ppermute | solution.py:48
  335.5 13.6 %collective-permute-start.67 = (bf16[64,1024]{1,0:T(8,128)(2,1)S(1)}, bf16[64,1024]{1,0:T(8,128)(2,1)S(1)}, u32[]{:S(2)}, u32[]{:S(2)}) collective-permute-start(bf16[64,1024]{1,0:T(8,128)(2,1)S(1)} %get-tuple-element.69), channel_id=1, source_target_pairs={{0,6},{2,4},{4,2},{6,0},{1,7},{3,5},{5,3},{7,1},{8,14},{10,12},{12... | collective-permute-start | bytes 393224 | tf_op jit(solution)/shard_map/ppermute | solution.py:48
  337.3 11.8 %collective-permute-start.68 = (bf16[64,1024]{1,0:T(8,128)(2,1)S(1)}, bf16[64,1024]{1,0:T(8,128)(2,1)S(1)}, u32[]{:S(2)}, u32[]{:S(2)}) collective-permute-start(bf16[64,1024]{1,0:T(8,128)(2,1)S(1)} %get-tuple-element.70), channel_id=1, source_target_pairs={{0,4},{2,6},{4,0},{6,2},{1,5},{3,7},{5,1},{7,3},{8,12},{10,14},{12... | collective-permute-start | bytes 393224 | tf_op jit(solution)/shard_map/ppermute | solution.py:48
  337.3 11.8 %collective-permute-start.69 = (bf16[64,1024]{1,0:T(8,128)(2,1)S(1)}, bf16[64,1024]{1,0:T(8,128)(2,1)S(1)}, u32[]{:S(2)}, u32[]{:S(2)}) collective-permute-start(bf16[64,1024]{1,0:T(8,128)(2,1)S(1)} %get-tuple-element.71), channel_id=1, source_target_pairs={{0,2},{2,0},{4,6},{6,4},{1,3},{3,1},{5,7},{7,5},{8,10},{10,8},{12,... | collective-permute-start | bytes 393224 | tf_op jit(solution)/shard_map/ppermute | solution.py:48
  352.6 12.6 %collective-permute-start.75 = (bf16[64,1024]{1,0:T(8,128)(2,1)}, bf16[64,1024]{1,0:T(8,128)(2,1)S(1)}, u32[]{:S(2)}, u32[]{:S(2)}) collective-permute-start(bf16[64,1024]{1,0:T(8,128)(2,1)} %get-tuple-element.75.refs_0_), channel_id=1, source_target_pairs={{0,2},{2,0},{4,6},{6,4},{1,3},{3,1},{5,7},{7,5},{8,10},{10,8},{12,... | collective-permute-start | bytes 393224 | tf_op jit(solution)/shard_map/ppermute | solution.py:48
  352.7 13.0 %collective-permute-start.76 = (bf16[64,1024]{1,0:T(8,128)(2,1)}, bf16[64,1024]{1,0:T(8,128)(2,1)S(1)}, u32[]{:S(2)}, u32[]{:S(2)}) collective-permute-start(bf16[64,1024]{1,0:T(8,128)(2,1)} %get-tuple-element.75.refs_0_), channel_id=1, source_target_pairs={{0,4},{2,6},{4,0},{6,2},{1,5},{3,7},{5,1},{7,3},{8,12},{10,14},{12... | collective-permute-start | bytes 393224 | tf_op jit(solution)/shard_map/ppermute | solution.py:48
  354.9 10.7 %collective-permute-start.77 = (bf16[64,1024]{1,0:T(8,128)(2,1)}, bf16[64,1024]{1,0:T(8,128)(2,1)S(1)}, u32[]{:S(2)}, u32[]{:S(2)}) collective-permute-start(bf16[64,1024]{1,0:T(8,128)(2,1)} %get-tuple-element.75.refs_0_), channel_id=1, source_target_pairs={{0,6},{2,4},{4,2},{6,0},{1,7},{3,5},{5,3},{7,1},{8,14},{10,12},{12... | collective-permute-start | bytes 393224 | tf_op jit(solution)/shard_map/ppermute | solution.py:48
  383.1 12.0 %collective-permute-start.78 = (bf16[4,64,1024]{2,1,0:T(8,128)(2,1)S(1)}, bf16[4,64,1024]{2,1,0:T(8,128)(2,1)S(1)}, u32[]{:S(2)}, u32[]{:S(2)}) collective-permute-start(bf16[4,64,1024]{2,1,0:T(8,128)(2,1)S(1)} %get-tuple-element.77), channel_id=1, source_target_pairs={{0,1},{1,0},{2,3},{3,2},{4,5},{5,4},{6,7},{7,6},{8,9},{9,8},{10,11... | collective-permute-start | bytes 1572872 | tf_op jit(solution)/shard_map/ppermute | solution.py:48
  396.0 16.2 %collective-permute-start.79 = (bf16[64,1024]{1,0:T(8,128)(2,1)S(1)}, bf16[64,1024]{1,0:T(8,128)(2,1)S(1)}, u32[]{:S(2)}, u32[]{:S(2)}) collective-permute-start(bf16[64,1024]{1,0:T(8,128)(2,1)S(1)} %get-tuple-element.84), channel_id=1, source_target_pairs={{0,8},{8,0},{16,24},{24,16},{1,9},{9,1},{17,25},{25,17},{2,10},{10... | collective-permute-start | bytes 393224 | tf_op jit(solution)/shard_map/ppermute | solution.py:48
  396.6 15.7 %collective-permute-start.80 = (bf16[64,1024]{1,0:T(8,128)(2,1)S(1)}, bf16[64,1024]{1,0:T(8,128)(2,1)S(1)}, u32[]{:S(2)}, u32[]{:S(2)}) collective-permute-start(bf16[64,1024]{1,0:T(8,128)(2,1)S(1)} %get-tuple-element.83), channel_id=1, source_target_pairs={{0,16},{8,24},{16,0},{24,8},{1,17},{9,25},{17,1},{25,9},{2,18},{10... | collective-permute-start | bytes 393224 | tf_op jit(solution)/shard_map/ppermute | solution.py:48
  397.8 14.5 %collective-permute-start.81 = (bf16[64,1024]{1,0:T(8,128)(2,1)S(1)}, bf16[64,1024]{1,0:T(8,128)(2,1)S(1)}, u32[]{:S(2)}, u32[]{:S(2)}) collective-permute-start(bf16[64,1024]{1,0:T(8,128)(2,1)S(1)} %get-tuple-element.82), channel_id=1, source_target_pairs={{0,24},{8,16},{16,8},{24,0},{1,25},{9,17},{17,9},{25,1},{2,26},{10... | collective-permute-start | bytes 393224 | tf_op jit(solution)/shard_map/ppermute | solution.py:48
  (93 other events, 610.2 us)

commit v2 on v1

--- a/solution.py
+++ b/solution.py
@@ -7,6 +7,7 @@
 from jax.experimental.pallas import tpu as pltpu
 from jax.sharding import PartitionSpec as P
 
+
 ITERS = 3
 
 ridge_weight = 1.0
@@ -30,11 +31,10 @@
     return first + lax.dot_general(lower, narrow, dims, preferred_element_type=f32)
 
 
-def call(body, outs, args, specs, name, scratch=(), flops=0, bytes_accessed=0, limit=None):
+def call(body, outs, args, specs, scratch=(), flops=0, bytes_accessed=0, limit=None):
     params = pltpu.CompilerParams(vmem_limit_bytes=limit) if limit else pltpu.CompilerParams()
     return pl.pallas_call(
         body,
-        name=name,
         out_shape=[jax.ShapeDtypeStruct(shape, dtype) for shape, dtype in outs],
         in_specs=specs,
         out_specs=[VMEM] * len(outs),
@@ -48,10 +48,8 @@
     return lax.ppermute(values, axis, [(at, at ^ mask) for at in range(size)])
 
 
-def stream_rows(design_ref, buffers, sems, first_sem, row_of, groups, per, tile, use):
+def stream_rows(design_ref, buffers, sems, row_of, steps, tile, use):
     depth = buffers.shape[0]
-    steps = groups * per
-    half = tile // 2
 
     def copy(step):
         slot = lax.rem(step, depth)
@@ -59,54 +57,45 @@
             design_ref.at[pl.ds(pl.multiple_of(row_of(step), tile), tile), :], buffers.at[slot], sems.at[slot]
         )
 
-    def copy_half(side):
-        return pltpu.make_async_copy(
-            design_ref.at[pl.ds(pl.multiple_of(row_of(0) + side * half, half), half), :],
-            buffers.at[0, pl.ds(side * half, half), :],
-            first_sem.at[side],
-        )
-
     def begin():
-        copy_half(0).start()
-        copy_half(1).start()
-        for step in range(1, min(depth, steps)):
+        for step in range(min(depth, steps)):
             copy(step).start()
 
     def run():
-        for group in range(groups):
-            if group == 0:
-                for side in range(2):
-                    copy_half(side).wait()
-                    use(0, side * half, buffers[0, side * half : (side + 1) * half, :])
-                if steps > depth:
-                    copy(depth).start()
-
-            def one(j, carry):
-                step = group * per + j
-                copy(step).wait()
-                use(group, pl.multiple_of(j * tile, tile), buffers[lax.rem(step, depth)])
-
-                @pl.when(step + depth < steps)
-                def _():
-                    copy(step + depth).start()
-
-                return carry
-
-            lax.fori_loop(1 if group == 0 else 0, per, one, 0)
+        def one(step, carry):
+            copy(step).wait()
+            use(step, buffers[lax.rem(step, depth)])
+
+            @pl.when(step + depth < steps)
+            def _():
+                copy(step + depth).start()
+
+            return carry
+
+        lax.fori_loop(0, steps, one, 0)
 
     return begin, run
 
 
-def place_shares(where, stacks, target, samples, rhs, width, turn):
+def place_shares(where, stacks, target, samples, rhs, width):
     for across in range(rhs):
         for mask in range(samples):
             share = (where[2] ^ across) * samples + (where[1] ^ mask)
-            start = pl.multiple_of(share * width, width)
-            piece = stacks[across][mask]
-            if turn:
-                target[pl.ds(start, width), :] = jnp.swapaxes(piece.astype(f32), 0, 1).astype(target.dtype)
-            else:
-                target[:, pl.ds(start, width)] = piece
+            target[:, pl.ds(pl.multiple_of(share * width, width), width)] = stacks[across][mask]
+
+
+def times_columns(block, left):
+    pieces = 4
+    width = left.shape[1] // pieces
+    cut = width * 3 // 4 if width * 3 % 1024 == 0 else width // 2
+    streamed, held = None, None
+    for start in range(0, pieces * width, width):
+        one = lax.dot_general(block[:, start : start + cut], left[:, start : start + cut], NT, preferred_element_type=f32)
+        span = slice(start + cut, start + width)
+        two = lax.dot_general(left[:, span], block[:, span], NT, preferred_element_type=f32)
+        streamed = one if streamed is None else streamed + one
+        held = two if held is None else held + two
+    return jnp.swapaxes(streamed, 0, 1) + held
 
 
 def forward_pass(where, stacks, design, masks, sizes):
@@ -121,19 +110,24 @@
     def body(where_ref, design_ref, *refs):
         stack_refs = refs[:rhs]
         outs = refs[rhs : rhs + len(masks)]
-        buffers, turned, sems, first_sem = refs[rhs + len(masks) :]
+        buffers, joined, sems = refs[rhs + len(masks) :]
         at = [where_ref[i] for i in range(3)]
 
         def row_of(step):
             return (at[0] ^ (masks[0] - step // per)) * chunk + lax.rem(step, per) * tile
 
-        def use(group, start, block):
-            out = jnp.dot(block, turned[...], preferred_element_type=f32)
-            outs[group][:, pl.ds(start, block.shape[0])] = jnp.swapaxes(out, 0, 1).astype(bf16)
-
-        begin, run = stream_rows(design_ref, buffers, sems, first_sem, row_of, len(masks), per, tile, use)
+        def use(step, block):
+            out = times_columns(block, joined[...]).astype(bf16)
+            start = pl.multiple_of(lax.rem(step, per) * tile, tile)
+            for group in range(len(masks)):
+
+                @pl.when(step // per == group)
+                def _(group=group):
+                    outs[group][:, pl.ds(start, tile)] = out
+
+        begin, run = stream_rows(design_ref, buffers, sems, row_of, len(masks) * per, tile, use)
         begin()
-        place_shares(at, stack_refs, turned, samples, rhs, width, True)
+        place_shares(at, stack_refs, joined, samples, rhs, width)
         run()
 
     work = len(masks) * chunk * depth
@@ -142,12 +136,10 @@
         [((cols, chunk), bf16)] * len(masks),
         (where, design, *stacks),
         [SMEM, HBM] + [VMEM] * rhs,
-        "forward",
         scratch=(
             pltpu.VMEM((4, tile, depth), bf16),
-            pltpu.VMEM((depth, cols), bf16),
+            pltpu.VMEM((cols, depth), bf16),
             pltpu.SemaphoreType.DMA((4,)),
-            pltpu.SemaphoreType.DMA((2,)),
         ),
         flops=2 * work * cols,
         bytes_accessed=2 * work,
@@ -169,24 +161,23 @@
         piece_refs = refs[:n]
         last = carried is not None
         if last:
-            start_ref, mine_ref, theirs_ref, buffers, total, sems, first_sem = refs[n:]
+            start_ref, mine_ref, theirs_ref, buffers, joined, sems, total = refs[n:]
         else:
-            total, buffers, sems, first_sem = refs[n:]
+            total, buffers, joined, sems = refs[n:]
         at = [where_ref[i] for i in range(3)]
 
         def row_of(step):
             return (at[0] ^ (masks[0] + step // per)) * chunk + lax.rem(step, per) * tile
 
-        def use(group, start, block):
-            left = piece_refs[group][:, pl.ds(start, block.shape[0])]
-            out = jnp.dot(left, block, preferred_element_type=f32)
-            if group == 0 and isinstance(start, int) and start == 0:
-                total[...] = start_ref[...] + out if last else out
-            else:
-                total[...] += out
-
-        begin, run = stream_rows(design_ref, buffers, sems, first_sem, row_of, n, per, tile, use)
+        def use(step, block):
+            left = joined[:, pl.ds(pl.multiple_of(step * tile, tile), tile)]
+            total[...] += jnp.dot(left, block, preferred_element_type=f32)
+
+        begin, run = stream_rows(design_ref, buffers, sems, row_of, n * per, tile, use)
         begin()
+        for group in range(n):
+            joined[:, group * chunk : (group + 1) * chunk] = piece_refs[group][...]
+        total[...] = start_ref[...] if last else jnp.zeros_like(total)
         run()
         if last:
             for side, out in ((0, mine_ref), (1, theirs_ref)):
@@ -196,7 +187,7 @@
 
     work = n * chunk * depth
     buffers = pltpu.VMEM((4, tile, depth), bf16)
-    sems = (pltpu.SemaphoreType.DMA((4,)), pltpu.SemaphoreType.DMA((2,)))
+    sems = (pltpu.VMEM((cols, n * chunk), bf16), pltpu.SemaphoreType.DMA((4,)))
     args = (where, design, *pieces)
     specs = [SMEM, HBM] + [VMEM] * n
     if carried is None:
@@ -206,9 +197,9 @@
         outs = [((samples, cols, width), bf16)] * 2
         args += (carried,)
         specs += [VMEM]
-        scratch = (buffers, pltpu.VMEM((cols, depth), f32), *sems)
-    return call(
-        body, outs, args, specs, "backward", scratch=scratch, flops=2 * work * cols, bytes_accessed=2 * work, limit=40 << 20
+        scratch = (buffers, *sems, pltpu.VMEM((cols, depth), f32))
+    return call(
+        body, outs, args, specs, scratch=scratch, flops=2 * work * cols, bytes_accessed=2 * work, limit=40 << 20
     )
 
 
@@ -219,12 +210,18 @@
 
 
 def sum_small(values, sizes):
-    for axis, size in zip(("rhs", "samples", "features"), (sizes[2], sizes[0], sizes[1])):
-        mask = 1
-        while mask < size:
-            values = values + exchange(values, axis, size, mask)
-            mask *= 2
+    for axis, size in zip(("samples", "features", "rhs"), sizes):
+        came = [exchange(values, axis, size, mask) for mask in range(1, size)]
+        for one in came:
+            values = values + one
     return values
+
+
+def sum_features(total, size):
+    whole = total
+    for mask in range(1, size):
+        whole = whole + exchange(total, "features", size, mask)
+    return whole
 
 
 def share_all(values, samples, rhs):
@@ -232,46 +229,47 @@
     return [stack] + [exchange(stack, "rhs", rhs, mask) for mask in range(1, rhs)]
 
 
-def sum_all(where, mine, theirs, sizes):
+def sum_all(mine, theirs, sizes):
     samples, feats, rhs = sizes
     pieces = merge(mine, theirs, samples, rhs, f32)
     total = pieces[0]
     for mask in range(1, samples):
         total = total + exchange(pieces[mask], "samples", samples, mask)
-    whole = total
-    for mask in range(1, feats):
-        whole = whole + exchange(total, "features", feats, mask)
-    return share_all(whole, samples, rhs)
+    return share_all(sum_features(total, feats), samples, rhs)
 
 
 def write_halves(where_ref, packed, mine_ref, theirs_ref):
-    samples, cols, width = mine_ref.shape
+    samples, _, width = mine_ref.shape
     for side, out in ((0, mine_ref), (1, theirs_ref)):
         for mask in range(samples):
             share = (where_ref[2] ^ side) * samples + (where_ref[1] ^ mask)
             out[mask] = packed[:, pl.ds(pl.multiple_of(share * width, width), width)]
 
 
-def first_products(where, res, basis, wide, sizes):
-    cols, rank = res.shape[0], basis.shape[1]
-
-    def body(where_ref, res_ref, basis_ref, mine_ref, theirs_ref, packed):
-        packed[...] = jnp.zeros_like(packed)
-        packed[:, :rank] = with_narrow(res_ref[...], basis_ref[...], (((1,), (0,)), ((), ())))
-        write_halves(where_ref, packed, mine_ref, theirs_ref)
-
-    return call(
-        body,
-        [((sizes[0], cols, wide // (sizes[0] * sizes[2])), f32)] * 2,
-        (where, res, basis),
-        [SMEM, VMEM, VMEM],
-        "first_products",
-        scratch=(pltpu.VMEM((cols, wide), f32),),
-    )
+def first_products(where, near, far, factor, width):
+    part, depth = near.shape
+    last_start = factor.shape[1] - width
+
+    def body(where_ref, near_ref, far_ref, factor_ref, out_ref, share_ref, sem):
+        start = pl.multiple_of(jnp.minimum(where_ref[1] * width, last_start), width)
+        copy = pltpu.make_async_copy(factor_ref.at[:, pl.ds(start, width)], share_ref, sem)
+        copy.start()
+        copy.wait()
+        for side, ref in ((0, near_ref), (1, far_ref)):
+            found = with_narrow(ref[...], share_ref[...], (((1,), (0,)), ((), ())))
+            out_ref[pl.ds(pl.multiple_of((where_ref[2] ^ side) * part, part), part), :] = found
+
+    return call(
+        body,
+        [((2 * part, width), f32)],
+        (where, near, far, factor),
+        [SMEM, VMEM, VMEM, HBM],
+        scratch=(pltpu.VMEM((depth, width), bf16), pltpu.SemaphoreType.DMA),
+    )[0]
 
 
 def first_update(where, stacks, res, basis, shrink, sizes):
-    samples, feats, rhs = sizes
+    samples, _, rhs = sizes
     cols, own = res.shape
     rank = basis.shape[1]
     width = stacks[0].shape[2]
@@ -281,9 +279,11 @@
         stack_refs = refs[:rhs]
         res_ref, basis_ref, shrink_ref, proj_ref, dir_ref, narrow_ref, packed = refs[rhs:]
         at = [where_ref[i] for i in range(3)]
-        place_shares(at, stack_refs, packed, samples, rhs, width, False)
-        proj = packed[:, :rank]
-        proj_ref[...] = proj
+        place_shares(at, stack_refs, packed, samples, rhs, width)
+        side = wide // rhs
+        for across in range(rhs):
+            proj_ref[:, across * (rank // rhs) : (across + 1) * (rank // rhs)] = packed[:, across * side : across * side + rank // rhs]
+        proj = proj_ref[...]
         direction = res_ref[...] + with_narrow(proj * shrink_ref[...], basis_ref[...], NT)
         dir_ref[...] = direction
         narrow_ref[...] = direction.astype(bf16)
@@ -293,7 +293,6 @@
         [((cols, rank), f32), ((cols, own), f32), ((cols, own), bf16)],
         (where, *stacks, res, basis, shrink),
         [SMEM] + [VMEM] * (rhs + 3),
-        "first_update",
         scratch=(pltpu.VMEM((cols, wide), f32),),
     )
 
@@ -325,7 +324,6 @@
         [((cols, own), f32)] + [((sizes[0], cols, wide // (sizes[0] * sizes[2])), f32)] * 2,
         (where, kept, *arrived, direction, res, basis),
         [SMEM] + [VMEM] * (n + 4),
-        "products",
         scratch=(pltpu.VMEM((cols, wide), f32),),
     )
 
@@ -336,16 +334,14 @@
     unit = lax.broadcasted_iota(jnp.int32, (size, size), 0) == lax.broadcasted_iota(jnp.int32, (size, size), 1)
     work = jnp.concatenate([matrix, unit.astype(f32)], axis=1)
     for k in range(size):
-        row = work[k : k + 1, :]
-        recip = 1.0 / row[:, k : k + 1]
-        column = work[:, k : k + 1]
-        scale = jnp.where(row_at == k, 1.0 - recip, column * recip)
-        work = work - scale * row
+        recip = 1.0 / work[k : k + 1, k : k + 1]
+        row = work[k : k + 1, :] * recip
+        work = jnp.where(row_at == k, row, work - work[:, k : k + 1] * row)
     return work[:, size:]
 
 
 def update(where, stacks, proj, direction, applied, res, basis, shrink, sizes):
-    samples, feats, rhs = sizes
+    samples, _, rhs = sizes
     cols, own = res.shape
     rank = basis.shape[1]
     width = stacks[0].shape[2]
@@ -356,7 +352,7 @@
         proj_ref, dir_ref, applied_ref, res_ref, basis_ref, shrink_ref, step_ref, new_res_ref = refs[rhs : rhs + 8]
         packed = refs[-1]
         at = [where_ref[i] for i in range(3)]
-        place_shares(at, stack_refs, packed, samples, rhs, width, False)
+        place_shares(at, stack_refs, packed, samples, rhs, width)
         gram = packed[:, rank : rank + cols]
         gram = 0.5 * (gram + jnp.swapaxes(gram, 0, 1))
         inv = inverse(gram)
@@ -384,7 +380,6 @@
         outs,
         (where, *stacks, proj, direction, applied, res, basis, shrink),
         [SMEM] + [VMEM] * (rhs + 6),
-        "update",
         scratch=(pltpu.VMEM((cols, wide), f32),),
     )
 
@@ -405,9 +400,7 @@
         gram_ref[:, :cols] = gram
         gram_ref[:, cols:] = exact(res_ref[...], direction_now, NT)
 
-    return call(
-        body, [((cols, chunk), bf16), ((cols, 2 * cols), f32)], (kept, *came, direction, res), [VMEM] * (n + 3), "gram_part"
-    )
+    return call(body, [((cols, chunk), bf16), ((cols, 2 * cols), f32)], (kept, *came, direction, res), [VMEM] * (n + 3))
 
 
 def last_step(grams):
@@ -418,7 +411,7 @@
         inv = inverse(0.5 * (gram + jnp.swapaxes(gram, 0, 1)))
         step_ref[...] = exact(gram_ref[:, cols:], 0.5 * (inv + jnp.swapaxes(inv, 0, 1)))
 
-    return call(body, [((cols, cols), f32)], (grams,), [VMEM], "last_step")[0]
+    return call(body, [((cols, cols), f32)], (grams,), [VMEM], flops=10**9)[0]
 
 
 def last_residual(where, kept, arrived, direction, res, step, part):
@@ -440,13 +433,12 @@
         [((part, own), bf16)] * 2,
         (where, kept, *arrived, direction, res, step),
         [SMEM] + [VMEM] * (n + 4),
-        "last_residual",
         scratch=(pltpu.VMEM((cols, own), f32),),
     )
 
 
 def collect(where, all_stacks, steps, sizes):
-    samples, feats, rhs = sizes
+    samples, _, rhs = sizes
     cols, width = all_stacks[0][0].shape[1:]
     part = cols // rhs
     count = len(all_stacks)
@@ -474,7 +466,6 @@
         [((part, depth), f32)],
         (where, *[one for stacks in all_stacks for one in stacks], *steps),
         [SMEM] + [VMEM] * (count * rhs + count),
-        "collect",
     )[0]
 
 
@@ -490,15 +481,18 @@
     unit = 128 * samples * rhs
     wide = -(-(rank + 4 * cols) // unit) * unit
 
-    def own_rows(block):
-        mine = lax.dynamic_slice_in_dim(block, (at_rhs * samples + at_sample) * own, own, 0)
-        theirs = lax.dynamic_slice_in_dim(block, ((1 - at_rhs) * samples + at_sample) * own, own, 0)
-        came = exchange(theirs, "rhs", rhs, 1)
-        return jnp.where(at_rhs == 0, jnp.concatenate([mine, came], 1), jnp.concatenate([came, mine], 1))
-
-    res = own_rows(right_side).T
-    basis = own_rows(factor)
-    proj_stacks = sum_all(where, *first_products(where, res, basis, wide, sizes), sizes)
+    share = at_rhs * samples + at_sample
+    other_share = (1 - at_rhs) * samples + at_sample
+    near = right_side.T
+    far = exchange(near, "rhs", rhs, 1)
+    found = sum_features(first_products(where, near, far, factor, wide // (samples * rhs)), feats)
+    proj_stacks = share_all(found, samples, rhs)
+    own_near = lax.dynamic_slice_in_dim(near, share * own, own, 1)
+    own_far = lax.dynamic_slice_in_dim(far, share * own, own, 1)
+    res = jnp.where(at_rhs == 0, jnp.concatenate([own_near, own_far]), jnp.concatenate([own_far, own_near]))
+    mine = lax.dynamic_slice_in_dim(factor, share * own, own, 0)
+    came = exchange(lax.dynamic_slice_in_dim(factor, other_share * own, own, 0), "rhs", rhs, 1)
+    basis = jnp.where(at_rhs == 0, jnp.concatenate([mine, came], 1), jnp.concatenate([came, mine], 1))
     proj, direction, narrow = first_update(where, proj_stacks, res, basis, shrink, sizes)
     all_stacks, steps = [], []
     for iteration in range(ITERS):
@@ -527,7 +521,7 @@
             same, other = last_residual(where, pieces[0], arrived, direction, res, step, col_share)
         else:
             applied, *halves = products(where, pieces[0], arrived, direction, res, basis, wide, sizes)
-            sums = sum_all(where, *halves, sizes)
+            sums = sum_all(*halves, sizes)
             step, res, proj, direction, narrow = update(
                 where, sums, proj, direction, applied, res, basis, shrink, sizes
             )

time: 436 us -> 419 us (0.961)
  waiting for transfers between devices: 98.4 us -> 87.5 us
    ppermute x86 -> x84, waiting for transfers between devices: 98.4 us -> 87.5 us  [exchange(): return lax.ppermute(values, axis, [(at, at ^ mask) for at in range(size)])]
    ppermute x86 -> x84, starting transfers between devices: 92.2 us -> 93.4 us  [exchange(): return lax.ppermute(values, axis, [(at, at ^ mask) for at in range(size)])]
  transfers between devices with their start and end apart: 86 -> 84, of which waited for: 55 -> 53; matrix products, arithmetic and copies ran while one was open for 1% -> 2% of each run, Pallas kernels for 14% -> 15%
where the time goes in v2:
time: 419 us; the launch traced here: 418 us
  Pallas kernels  205 us (49%)
  starting transfers between devices  93.4 us (22%)
  waiting for transfers between devices  87.5 us (21%)
  local copies, waits for them, and re-layouts  14.9 us (4%)
  other arithmetic  14.9 us (4%)
    pallas_call x22, Pallas kernels, call(): pl.pallas_call(body, out_shape=[jax.ShapeDtypeStruct(shape, dtype) for sh...  205 us
    ppermute x84, starting transfers between devices, exchange(): return lax.ppermute(values, axis, [(at, at ^ mask) for at in range(size)])  93.4 us
    ppermute x84, waiting for transfers between devices, exchange(): return lax.ppermute(values, axis, [(at, at ^ mask) for at in range(size)])  87.5 us
  transfers between devices with their start and end apart: 84, of which 53 were waited for; matrix products, arithmetic and copies ran while one was open for 2% of the time, Pallas kernels for 15%

profile of v2, /device:TPU:0, one launch (start us, length us, event | category | flops | bytes accessed | tf_op | source)
XLA Modules:
  0.0 417.7 jit_solution(4018725703354854277)
XLA Ops:
  5.7 5.0 %shard_map.59 = f32[64,128]{1,0:T(8,128)} custom-call(s32[3]{0:T(128)} %pad_add_fusion.where_ref, f32[32,8192]{1,0:T(8,128)} %bitcast.99, f32[32,8192]{1,0:T(8,128)} %copy-done.11, bf16[8192,384]{1,0:T(8,128)(2,1)} %factor_ref.1), custom_call_target="tpu_custom_call" | custom-call | tf_op jit(solution)/shard_map/pallas_call | solution.py:36
  10.8 3.1 collective-permute-start.1
  33.5 3.4 shard_map.60
  49.0 17.8 %shard_map.62 = (bf16[64,1024]{1,0:T(8,128)(2,1)S(1)}, bf16[64,1024]{1,0:T(8,128)(2,1)S(1)}, bf16[64,1024]{1,0:T(8,128)(2,1)S(1)}) custom-call(s32[3]{0:T(128)S(1)} %copy-done.7, bf16[4096,8192]{1,0:T(8,128)(2,1)} %design_ref.23, bf16[4,64,1024]{2,1,0:T(8,128)(2,1)S(1)} %pad_maximum_fusion.refs_0_, bf16[4,64,1024]{2,1,0:T(8,128)(2,1)S(1)} %collective-permute-done.12.refs_1_), custom_call_target="tpu_custom_call" | custom-call | flops 3221225472 | bytes 50331648 | tf_op jit(solution)/shard_map/pallas_call | solution.py:36
  67.3 3.9 collective-permute-start.15
  71.2 7.8 %shard_map.61 = bf16[64,1024]{1,0:T(8,128)(2,1)S(1)} custom-call(s32[3]{0:T(128)S(1)} %copy-done.7, bf16[4096,8192]{1,0:T(8,128)(2,1)} %design_ref.23, bf16[4,64,1024]{2,1,0:T(8,128)(2,1)S(1)} %pad_maximum_fusion.refs_0_, bf16[4,64,1024]{2,1,0:T(8,128)(2,1)S(1)} %collective-permute-done.12.refs_1_), custom_call_target="tpu_custom_call" | custom-call | flops 1073741824 | bytes 16777216 | tf_op jit(solution)/shard_map/pallas_call | solution.py:36
  83.6 7.3 %shard_map.63.refs_3_ = f32[64,8192]{1,0:T(8,128)S(1)} custom-call(s32[3]{0:T(128)S(1)} %copy-done.7, bf16[4096,8192]{1,0:T(8,128)(2,1)} %design_ref.23, bf16[64,1024]{1,0:T(8,128)(2,1)S(1)} %add_convert_fusion.10.refs_0_), custom_call_target="tpu_custom_call" | custom-call | flops 1073741824 | bytes 16777216 | tf_op jit(solution)/shard_map/pallas_call | solution.py:36
  91.8 17.2 %shard_map.64 = (bf16[4,64,1024]{2,1,0:T(8,128)(2,1)S(1)}, bf16[4,64,1024]{2,1,0:T(8,128)(2,1)S(1)}) custom-call(s32[3]{0:T(128)S(1)} %copy-done.7, bf16[4096,8192]{1,0:T(8,128)(2,1)} %design_ref.23, bf16[64,1024]{1,0:T(8,128)(2,1)S(1)} %collective-permute-done.16.refs_0_, bf16[64,1024]{1,0:T(8,128)(2,1)S(1)} %collective-permute-done.17.refs_1_, ...), custom_call_target="tpu_custom_call" | custom-call | flops 3221225472 | bytes 50331648 | tf_op jit(solution)/shard_map/pallas_call | solution.py:36
  117.8 3.6 collective-permute-done.21.refs_1_
  122.1 4.2 %shard_map.65 = (f32[64,1024]{1,0:T(8,128)}, f32[4,64,128]{2,1,0:T(8,128)}, f32[4,64,128]{2,1,0:T(8,128)}) custom-call(s32[3]{0:T(128)} %pad_add_fusion.where_ref, f32[64,1024]{1,0:T(8,128)} %get-tuple-element.89.kept_ref, bf16[64,1024]{1,0:T(8,128)(2,1)} %copy-done.18, bf16[64,1024]{1,0:T(8,128)(2,1)} %copy-done.20, bf16[64,1024]{1,0:T(8,128)(2,1)} %copy-done.22, ...), custom_call_target="tpu_custom_call" | custom-call | tf_op jit(solution)/shard_map/pallas_call | solution.py:36
  154.3 10.9 %shard_map.66 = (f32[64,64]{1,0:T(8,128)}, f32[64,1024]{1,0:T(8,128)}, f32[64,768]{1,0:T(8,128)}, f32[64,1024]{1,0:T(8,128)}, bf16[64,1024]{1,0:T(8,128)(2,1)}) custom-call(s32[3]{0:T(128)} %pad_add_fusion.where_ref, f32[4,64,128]{2,1,0:T(8,128)} %copy-done.13, f32[4,64,128]{2,1,0:T(8,128)} %copy-done.25, f32[64,768]{1,0:T(8,128)} %get-tuple-element.48.refs_2_, ...), custom_call_target="tpu_custom_call" | custom-call | tf_op jit(solution)/shard_map/pallas_call | solution.py:36
  177.0 17.8 %shard_map.68 = (bf16[64,1024]{1,0:T(8,128)(2,1)S(1)}, bf16[64,1024]{1,0:T(8,128)(2,1)S(1)}, bf16[64,1024]{1,0:T(8,128)(2,1)S(1)}) custom-call(s32[3]{0:T(128)S(1)} %copy-done.8, bf16[4096,8192]{1,0:T(8,128)(2,1)} %design_ref.23, bf16[4,64,1024]{2,1,0:T(8,128)(2,1)S(1)} %pad_maximum_fusion.1.refs_0_.refs_2_, ...), custom_call_target="tpu_custom_call" | custom-call | flops 3221225472 | bytes 50331648 | tf_op jit(solution)/shard_map/pallas_call | solution.py:36
  199.3 7.8 %shard_map.67 = bf16[64,1024]{1,0:T(8,128)(2,1)S(1)} custom-call(s32[3]{0:T(128)S(1)} %copy-done.8, bf16[4096,8192]{1,0:T(8,128)(2,1)} %design_ref.23, bf16[4,64,1024]{2,1,0:T(8,128)(2,1)S(1)} %pad_maximum_fusion.1.refs_0_.refs_2_, bf16[4,64,1024]{2,1,0:T(8,128)(2,1)S(1)} %collective-permute-done.37.refs_1_.refs_3_), custom_call_target="tpu_custom_call" | custom-call | flops 1073741824 | bytes 16777216 | tf_op jit(solution)/shard_map/pallas_call | solution.py:36
  213.0 7.3 %shard_map.69.refs_3_ = f32[64,8192]{1,0:T(8,128)S(1)} custom-call(s32[3]{0:T(128)S(1)} %copy-done.8, bf16[4096,8192]{1,0:T(8,128)(2,1)} %design_ref.23, bf16[64,1024]{1,0:T(8,128)(2,1)S(1)} %add_convert_fusion.6.refs_0_), custom_call_target="tpu_custom_call" | custom-call | flops 1073741824 | bytes 16777216 | tf_op jit(solution)/shard_map/pallas_call | solution.py:36
  221.5 17.2 %shard_map.70 = (bf16[4,64,1024]{2,1,0:T(8,128)(2,1)S(1)}, bf16[4,64,1024]{2,1,0:T(8,128)(2,1)S(1)}) custom-call(s32[3]{0:T(128)S(1)} %copy-done.8, bf16[4096,8192]{1,0:T(8,128)(2,1)} %design_ref.23, bf16[64,1024]{1,0:T(8,128)(2,1)S(1)} %collective-permute-done.41.refs_0_, bf16[64,1024]{1,0:T(8,128)(2,1)S(1)} %collective-permute-done.42.refs_1_, ...), custom_call_target="tpu_custom_call" | custom-call | flops 3221225472 | bytes 50331648 | tf_op jit(solution)/shard_map/pallas_call | solution.py:36
  247.5 3.6 collective-permute-done.46.refs_1_
  251.8 4.2 %shard_map.71 = (f32[64,1024]{1,0:T(8,128)}, f32[4,64,128]{2,1,0:T(8,128)}, f32[4,64,128]{2,1,0:T(8,128)}) custom-call(s32[3]{0:T(128)} %pad_add_fusion.where_ref, f32[64,1024]{1,0:T(8,128)} %get-tuple-element.85.kept_ref, bf16[64,1024]{1,0:T(8,128)(2,1)} %copy-done.19, bf16[64,1024]{1,0:T(8,128)(2,1)} %copy-done.21, bf16[64,1024]{1,0:T(8,128)(2,1)} %copy-done.23, ...), custom_call_target="tpu_custom_call" | custom-call | tf_op jit(solution)/shard_map/pallas_call | solution.py:36
  283.1 10.9 %shard_map.72 = (f32[64,64]{1,0:T(8,128)}, f32[64,1024]{1,0:T(8,128)}, f32[64,768]{1,0:T(8,128)}, f32[64,1024]{1,0:T(8,128)}, bf16[64,1024]{1,0:T(8,128)(2,1)}) custom-call(s32[3]{0:T(128)} %pad_add_fusion.where_ref, f32[4,64,128]{2,1,0:T(8,128)} %copy-done.12, f32[4,64,128]{2,1,0:T(8,128)} %copy-done.24, f32[64,768]{1,0:T(8,128)} %get-tuple-element.60.refs_2_, ...), custom_call_target="tpu_custom_call" | custom-call | tf_op jit(solution)/shard_map/pallas_call | solution.py:36
  305.8 17.8 %shard_map.74 = (bf16[64,1024]{1,0:T(8,128)(2,1)S(1)}, bf16[64,1024]{1,0:T(8,128)(2,1)S(1)}, bf16[64,1024]{1,0:T(8,128)(2,1)S(1)}) custom-call(s32[3]{0:T(128)S(1)} %copy-done.9, bf16[4096,8192]{1,0:T(8,128)(2,1)} %design_ref.23, bf16[4,64,1024]{2,1,0:T(8,128)(2,1)S(1)} %pad_maximum_fusion.2.refs_0_.refs_4_, ...), custom_call_target="tpu_custom_call" | custom-call | flops 3221225472 | bytes 50331648 | tf_op jit(solution)/shard_map/pallas_call | solution.py:36
  328.0 8.0 %shard_map.73.kept_ref = bf16[64,1024]{1,0:T(8,128)(2,1)S(1)} custom-call(s32[3]{0:T(128)S(1)} %copy-done.9, bf16[4096,8192]{1,0:T(8,128)(2,1)} %design_ref.23, bf16[4,64,1024]{2,1,0:T(8,128)(2,1)S(1)} %pad_maximum_fusion.2.refs_0_.refs_4_, bf16[4,64,1024]{2,1,0:T(8,128)(2,1)S(1)} %collective-permute-done.62.refs_1_.refs_5_), custom_call_target="tpu_custom_call" | custom-call | flops 1073741824 | bytes 16777216 | tf_op jit(solution)/shard_map/pallas_call | solution.py:36
  346.0 7.3 %shard_map.78.refs_3_ = f32[64,8192]{1,0:T(8,128)S(1)} custom-call(s32[3]{0:T(128)S(1)} %copy-done.9, bf16[4096,8192]{1,0:T(8,128)(2,1)} %design_ref.23, bf16[64,1024]{1,0:T(8,128)(2,1)S(1)} %copy-done.10), custom_call_target="tpu_custom_call" | custom-call | flops 1073741824 | bytes 16777216 | tf_op jit(solution)/shard_map/pallas_call | solution.py:36
  353.8 17.2 %shard_map.79 = (bf16[4,64,1024]{2,1,0:T(8,128)(2,1)S(1)}, bf16[4,64,1024]{2,1,0:T(8,128)(2,1)S(1)}) custom-call(s32[3]{0:T(128)S(1)} %copy-done.9, bf16[4096,8192]{1,0:T(8,128)(2,1)} %design_ref.23, bf16[64,1024]{1,0:T(8,128)(2,1)S(1)} %collective-permute-done.73.refs_0_, bf16[64,1024]{1,0:T(8,128)(2,1)S(1)} %collective-permute-done.74.refs_1_, ...), custom_call_target="tpu_custom_call" | custom-call | flops 3221225472 | bytes 50331648 | tf_op jit(solution)/shard_map/pallas_call | solution.py:36
  391.9 7.3 %shard_map.76.refs_8_.refs_5_ = f32[64,64]{1,0:T(8,128)} custom-call(f32[64,128]{1,0:T(8,128)} %add.283.gram_ref), custom_call_target="tpu_custom_call" | custom-call | flops 1000000000 | tf_op jit(solution)/shard_map/pallas_call | solution.py:36
  408.2 3.8 shard_map.77
  (271 shorter events, 201.5 us)
Async XLA Ops:
  2.7 24.0 %collective-permute-start.8 = (bf16[1024,384]{1,0:T(8,128)(2,1)S(1)}, bf16[1024,384]{1,0:T(8,128)(2,1)S(1)}, u32[]{:S(2)}, u32[]{:S(2)}) collective-permute-start(bf16[1024,384]{1,0:T(8,128)(2,1)S(1)} %get-tuple-element.77), channel_id=1, source_target_pairs={{0,1},{1,0},{2,3},{3,2},{4,5},{5,4},{6,7},{7,6},{8,9},{9,8},{10,11... | collective-permute-start | bytes 2359304 | tf_op jit(solution)/shard_map/ppermute | solution.py:48
  37.3 8.6 %collective-permute-start.10 = (bf16[64,1024]{1,0:T(8,128)(2,1)}, bf16[64,1024]{1,0:T(8,128)(2,1)S(1)}, u32[]{:S(2)}, u32[]{:S(2)}) collective-permute-start(bf16[64,1024]{1,0:T(8,128)(2,1)} %get-tuple-element.39), channel_id=1, source_target_pairs={{0,16},{8,24},{16,0},{24,8},{1,17},{9,25},{17,1},{25,9},{2,18},{10... | collective-permute-start | bytes 393224 | tf_op jit(solution)/shard_map/ppermute | solution.py:48
  66.8 12.2 %collective-permute-start.13 = (bf16[64,1024]{1,0:T(8,128)(2,1)S(1)}, bf16[64,1024]{1,0:T(8,128)(2,1)S(1)}, u32[]{:S(2)}, u32[]{:S(2)}) collective-permute-start(bf16[64,1024]{1,0:T(8,128)(2,1)S(1)} %get-tuple-element.40), channel_id=1, source_target_pairs={{0,6},{2,4},{4,2},{6,0},{1,7},{3,5},{5,3},{7,1},{8,14},{10,12},{12... | collective-permute-start | bytes 393224 | tf_op jit(solution)/shard_map/ppermute | solution.py:48
  67.3 11.8 %collective-permute-start.14 = (bf16[64,1024]{1,0:T(8,128)(2,1)S(1)}, bf16[64,1024]{1,0:T(8,128)(2,1)S(1)}, u32[]{:S(2)}, u32[]{:S(2)}) collective-permute-start(bf16[64,1024]{1,0:T(8,128)(2,1)S(1)} %get-tuple-element.41), channel_id=1, source_target_pairs={{0,4},{2,6},{4,0},{6,2},{1,5},{3,7},{5,1},{7,3},{8,12},{10,14},{12... | collective-permute-start | bytes 393224 | tf_op jit(solution)/shard_map/ppermute | solution.py:48
  67.3 11.8 %collective-permute-start.15 = (bf16[64,1024]{1,0:T(8,128)(2,1)S(1)}, bf16[64,1024]{1,0:T(8,128)(2,1)S(1)}, u32[]{:S(2)}, u32[]{:S(2)}) collective-permute-start(bf16[64,1024]{1,0:T(8,128)(2,1)S(1)} %get-tuple-element.42), channel_id=1, source_target_pairs={{0,2},{2,0},{4,6},{6,4},{1,3},{3,1},{5,7},{7,5},{8,10},{10,8},{12,... | collective-permute-start | bytes 393224 | tf_op jit(solution)/shard_map/ppermute | solution.py:48
  79.2 11.7 %collective-permute-start.16 = (bf16[64,1024]{1,0:T(8,128)(2,1)S(1)}, bf16[64,1024]{1,0:T(8,128)(2,1)S(1)}, u32[]{:S(2)}, u32[]{:S(2)}) collective-permute-start(bf16[64,1024]{1,0:T(8,128)(2,1)S(1)} %add_convert_fusion.10.refs_0_), channel_id=1, source_target_pairs={{0,2},{2,0},{4,6},{6,4},{1,3},{3,1},{5,7},{7,5},{8,10},{10,8},{12,... | collective-permute-start | bytes 393224 | tf_op jit(solution)/shard_map/ppermute | solution.py:48
  79.2 12.6 %collective-permute-start.17 = (bf16[64,1024]{1,0:T(8,128)(2,1)S(1)}, bf16[64,1024]{1,0:T(8,128)(2,1)S(1)}, u32[]{:S(2)}, u32[]{:S(2)}) collective-permute-start(bf16[64,1024]{1,0:T(8,128)(2,1)S(1)} %add_convert_fusion.10.refs_0_), channel_id=1, source_target_pairs={{0,4},{2,6},{4,0},{6,2},{1,5},{3,7},{5,1},{7,3},{8,12},{10,14},{12... | collective-permute-start | bytes 393224 | tf_op jit(solution)/shard_map/ppermute | solution.py:48
  82.0 9.8 %collective-permute-start.18 = (bf16[64,1024]{1,0:T(8,128)(2,1)S(1)}, bf16[64,1024]{1,0:T(8,128)(2,1)S(1)}, u32[]{:S(2)}, u32[]{:S(2)}) collective-permute-start(bf16[64,1024]{1,0:T(8,128)(2,1)S(1)} %add_convert_fusion.10.refs_0_), channel_id=1, source_target_pairs={{0,6},{2,4},{4,2},{6,0},{1,7},{3,5},{5,3},{7,1},{8,14},{10,12},{12... | collective-permute-start | bytes 393224 | tf_op jit(solution)/shard_map/ppermute | solution.py:48
  194.8 12.2 %collective-permute-start.38 = (bf16[64,1024]{1,0:T(8,128)(2,1)S(1)}, bf16[64,1024]{1,0:T(8,128)(2,1)S(1)}, u32[]{:S(2)}, u32[]{:S(2)}) collective-permute-start(bf16[64,1024]{1,0:T(8,128)(2,1)S(1)} %get-tuple-element.51), channel_id=1, source_target_pairs={{0,6},{2,4},{4,2},{6,0},{1,7},{3,5},{5,3},{7,1},{8,14},{10,12},{12... | collective-permute-start | bytes 393224 | tf_op jit(solution)/shard_map/ppermute | solution.py:48
  196.3 12.2 %collective-permute-start.39 = (bf16[64,1024]{1,0:T(8,128)(2,1)S(1)}, bf16[64,1024]{1,0:T(8,128)(2,1)S(1)}, u32[]{:S(2)}, u32[]{:S(2)}) collective-permute-start(bf16[64,1024]{1,0:T(8,128)(2,1)S(1)} %get-tuple-element.52), channel_id=1, source_target_pairs={{0,4},{2,6},{4,0},{6,2},{1,5},{3,7},{5,1},{7,3},{8,12},{10,14},{12... | collective-permute-start | bytes 393224 | tf_op jit(solution)/shard_map/ppermute | solution.py:48
  196.5 12.0 %collective-permute-start.40 = (bf16[64,1024]{1,0:T(8,128)(2,1)S(1)}, bf16[64,1024]{1,0:T(8,128)(2,1)S(1)}, u32[]{:S(2)}, u32[]{:S(2)}) collective-permute-start(bf16[64,1024]{1,0:T(8,128)(2,1)S(1)} %get-tuple-element.53), channel_id=1, source_target_pairs={{0,2},{2,0},{4,6},{6,4},{1,3},{3,1},{5,7},{7,5},{8,10},{10,8},{12,... | collective-permute-start | bytes 393224 | tf_op jit(solution)/shard_map/ppermute | solution.py:48
  208.6 11.7 %collective-permute-start.41 = (bf16[64,1024]{1,0:T(8,128)(2,1)S(1)}, bf16[64,1024]{1,0:T(8,128)(2,1)S(1)}, u32[]{:S(2)}, u32[]{:S(2)}) collective-permute-start(bf16[64,1024]{1,0:T(8,128)(2,1)S(1)} %add_convert_fusion.6.refs_0_), channel_id=1, source_target_pairs={{0,2},{2,0},{4,6},{6,4},{1,3},{3,1},{5,7},{7,5},{8,10},{10,8},{12,... | collective-permute-start | bytes 393224 | tf_op jit(solution)/shard_map/ppermute | solution.py:48
  208.6 12.8 %collective-permute-start.42 = (bf16[64,1024]{1,0:T(8,128)(2,1)S(1)}, bf16[64,1024]{1,0:T(8,128)(2,1)S(1)}, u32[]{:S(2)}, u32[]{:S(2)}) collective-permute-start(bf16[64,1024]{1,0:T(8,128)(2,1)S(1)} %add_convert_fusion.6.refs_0_), channel_id=1, source_target_pairs={{0,4},{2,6},{4,0},{6,2},{1,5},{3,7},{5,1},{7,3},{8,12},{10,14},{12... | collective-permute-start | bytes 393224 | tf_op jit(solution)/shard_map/ppermute | solution.py:48
  210.6 10.9 %collective-permute-start.43 = (bf16[64,1024]{1,0:T(8,128)(2,1)S(1)}, bf16[64,1024]{1,0:T(8,128)(2,1)S(1)}, u32[]{:S(2)}, u32[]{:S(2)}) collective-permute-start(bf16[64,1024]{1,0:T(8,128)(2,1)S(1)} %add_convert_fusion.6.refs_0_), channel_id=1, source_target_pairs={{0,6},{2,4},{4,2},{6,0},{1,7},{3,5},{5,3},{7,1},{8,14},{10,12},{12... | collective-permute-start | bytes 393224 | tf_op jit(solution)/shard_map/ppermute | solution.py:48
  323.6 13.2 %collective-permute-start.63 = (bf16[64,1024]{1,0:T(8,128)(2,1)S(1)}, bf16[64,1024]{1,0:T(8,128)(2,1)S(1)}, u32[]{:S(2)}, u32[]{:S(2)}) collective-permute-start(bf16[64,1024]{1,0:T(8,128)(2,1)S(1)} %get-tuple-element.65), channel_id=1, source_target_pairs={{0,6},{2,4},{4,2},{6,0},{1,7},{3,5},{5,3},{7,1},{8,14},{10,12},{12... | collective-permute-start | bytes 393224 | tf_op jit(solution)/shard_map/ppermute | solution.py:48
  326.0 11.2 %collective-permute-start.64 = (bf16[64,1024]{1,0:T(8,128)(2,1)S(1)}, bf16[64,1024]{1,0:T(8,128)(2,1)S(1)}, u32[]{:S(2)}, u32[]{:S(2)}) collective-permute-start(bf16[64,1024]{1,0:T(8,128)(2,1)S(1)} %get-tuple-element.66), channel_id=1, source_target_pairs={{0,4},{2,6},{4,0},{6,2},{1,5},{3,7},{5,1},{7,3},{8,12},{10,14},{12... | collective-permute-start | bytes 393224 | tf_op jit(solution)/shard_map/ppermute | solution.py:48
  326.0 11.2 %collective-permute-start.65 = (bf16[64,1024]{1,0:T(8,128)(2,1)S(1)}, bf16[64,1024]{1,0:T(8,128)(2,1)S(1)}, u32[]{:S(2)}, u32[]{:S(2)}) collective-permute-start(bf16[64,1024]{1,0:T(8,128)(2,1)S(1)} %get-tuple-element.67), channel_id=1, source_target_pairs={{0,2},{2,0},{4,6},{6,4},{1,3},{3,1},{5,7},{7,5},{8,10},{10,8},{12,... | collective-permute-start | bytes 393224 | tf_op jit(solution)/shard_map/ppermute | solution.py:48
  340.7 12.6 %collective-permute-start.73 = (bf16[64,1024]{1,0:T(8,128)(2,1)}, bf16[64,1024]{1,0:T(8,128)(2,1)S(1)}, u32[]{:S(2)}, u32[]{:S(2)}) collective-permute-start(bf16[64,1024]{1,0:T(8,128)(2,1)} %get-tuple-element.71.refs_0_), channel_id=1, source_target_pairs={{0,2},{2,0},{4,6},{6,4},{1,3},{3,1},{5,7},{7,5},{8,10},{10,8},{12,... | collective-permute-start | bytes 393224 | tf_op jit(solution)/shard_map/ppermute | solution.py:48
  340.7 13.2 %collective-permute-start.74 = (bf16[64,1024]{1,0:T(8,128)(2,1)}, bf16[64,1024]{1,0:T(8,128)(2,1)S(1)}, u32[]{:S(2)}, u32[]{:S(2)}) collective-permute-start(bf16[64,1024]{1,0:T(8,128)(2,1)} %get-tuple-element.71.refs_0_), channel_id=1, source_target_pairs={{0,4},{2,6},{4,0},{6,2},{1,5},{3,7},{5,1},{7,3},{8,12},{10,14},{12... | collective-permute-start | bytes 393224 | tf_op jit(solution)/shard_map/ppermute | solution.py:48
  343.6 10.2 %collective-permute-start.75 = (bf16[64,1024]{1,0:T(8,128)(2,1)}, bf16[64,1024]{1,0:T(8,128)(2,1)S(1)}, u32[]{:S(2)}, u32[]{:S(2)}) collective-permute-start(bf16[64,1024]{1,0:T(8,128)(2,1)} %get-tuple-element.71.refs_0_), channel_id=1, source_target_pairs={{0,6},{2,4},{4,2},{6,0},{1,7},{3,5},{5,3},{7,1},{8,14},{10,12},{12... | collective-permute-start | bytes 393224 | tf_op jit(solution)/shard_map/ppermute | solution.py:48
  371.0 15.9 %collective-permute-start.76 = (bf16[4,64,1024]{2,1,0:T(8,128)(2,1)S(1)}, bf16[4,64,1024]{2,1,0:T(8,128)(2,1)S(1)}, u32[]{:S(2)}, u32[]{:S(2)}) collective-permute-start(bf16[4,64,1024]{2,1,0:T(8,128)(2,1)S(1)} %get-tuple-element.73), channel_id=1, source_target_pairs={{0,1},{1,0},{2,3},{3,2},{4,5},{5,4},{6,7},{7,6},{8,9},{9,8},{10,11... | collective-permute-start | bytes 1572872 | tf_op jit(solution)/shard_map/ppermute | solution.py:48
  387.7 11.4 %collective-permute-start.77 = (bf16[64,1024]{1,0:T(8,128)(2,1)S(1)}, bf16[64,1024]{1,0:T(8,128)(2,1)S(1)}, u32[]{:S(2)}, u32[]{:S(2)}) collective-permute-start(bf16[64,1024]{1,0:T(8,128)(2,1)S(1)} %get-tuple-element.80), channel_id=1, source_target_pairs={{0,8},{8,0},{16,24},{24,16},{1,9},{9,1},{17,25},{25,17},{2,10},{10... | collective-permute-start | bytes 393224 | tf_op jit(solution)/shard_map/ppermute | solution.py:48
  389.0 10.2 %collective-permute-start.78 = (bf16[64,1024]{1,0:T(8,128)(2,1)S(1)}, bf16[64,1024]{1,0:T(8,128)(2,1)S(1)}, u32[]{:S(2)}, u32[]{:S(2)}) collective-permute-start(bf16[64,1024]{1,0:T(8,128)(2,1)S(1)} %get-tuple-element.79), channel_id=1, source_target_pairs={{0,16},{8,24},{16,0},{24,8},{1,17},{9,25},{17,1},{25,9},{2,18},{10... | collective-permute-start | bytes 393224 | tf_op jit(solution)/shard_map/ppermute | solution.py:48
  389.8 9.4 %collective-permute-start.79 = (bf16[64,1024]{1,0:T(8,128)(2,1)S(1)}, bf16[64,1024]{1,0:T(8,128)(2,1)S(1)}, u32[]{:S(2)}, u32[]{:S(2)}) collective-permute-start(bf16[64,1024]{1,0:T(8,128)(2,1)S(1)} %get-tuple-element.78), channel_id=1, source_target_pairs={{0,24},{8,16},{16,8},{24,0},{1,25},{9,17},{17,9},{25,1},{2,26},{10... | collective-permute-start | bytes 393224 | tf_op jit(solution)/shard_map/ppermute | solution.py:48
  (92 other events, 557.4 us)

commit v3 on v2

--- a/solution.py
+++ b/solution.py
@@ -27,8 +27,8 @@
 def with_narrow(values, narrow, dims):
     upper = values.astype(bf16)
     lower = (values - upper.astype(f32)).astype(bf16)
-    first = lax.dot_general(upper, narrow, dims, preferred_element_type=f32)
-    return first + lax.dot_general(lower, narrow, dims, preferred_element_type=f32)
+    both = lax.dot_general(jnp.concatenate([upper, lower]), narrow, dims, preferred_element_type=f32)
+    return both[: values.shape[0]] + both[values.shape[0] :]
 
 
 def call(body, outs, args, specs, scratch=(), flops=0, bytes_accessed=0, limit=None):
@@ -152,7 +152,7 @@
     rows, depth = design.shape
     cols = pieces[0].shape[0]
     chunk = rows // feats
-    tile = min(256, chunk)
+    tile = min(128, chunk)
     per = chunk // tile
     width = depth // (samples * rhs)
     n = len(masks)
@@ -186,8 +186,8 @@
                     out[mask] = total[:, pl.ds(pl.multiple_of(share * width, width), width)].astype(bf16)
 
     work = n * chunk * depth
-    buffers = pltpu.VMEM((4, tile, depth), bf16)
-    sems = (pltpu.VMEM((cols, n * chunk), bf16), pltpu.SemaphoreType.DMA((4,)))
+    buffers = pltpu.VMEM((8, tile, depth), bf16)
+    sems = (pltpu.VMEM((cols, n * chunk), bf16), pltpu.SemaphoreType.DMA((8,)))
     args = (where, design, *pieces)
     specs = [SMEM, HBM] + [VMEM] * n
     if carried is None:
@@ -255,9 +255,10 @@
         copy = pltpu.make_async_copy(factor_ref.at[:, pl.ds(start, width)], share_ref, sem)
         copy.start()
         copy.wait()
-        for side, ref in ((0, near_ref), (1, far_ref)):
-            found = with_narrow(ref[...], share_ref[...], (((1,), (0,)), ((), ())))
-            out_ref[pl.ds(pl.multiple_of((where_ref[2] ^ side) * part, part), part), :] = found
+        both = jnp.concatenate([near_ref[...], far_ref[...]])
+        found = with_narrow(both, share_ref[...], (((1,), (0,)), ((), ())))
+        for side in range(2):
+            out_ref[pl.ds(pl.multiple_of((where_ref[2] ^ side) * part, part), part), :] = found[side * part : (side + 1) * part]
 
     return call(
         body,
@@ -312,11 +313,12 @@
         applied = applied + ridge_weight * direction_now
         applied_ref[...] = applied
         packed[...] = jnp.zeros_like(packed)
-        packed[:, rank : rank + cols] = exact(direction_now, applied, NT)
+        found = exact(jnp.concatenate([direction_now, applied, residual]), applied, NT)
+        packed[:, rank : rank + cols] = found[:cols]
         packed[:, rank + cols : rank + 2 * cols] = exact(residual, direction_now, NT)
         packed[:, :rank] = with_narrow(applied, basis_ref[...], (((1,), (0,)), ((), ())))
-        packed[:, rank + 2 * cols : rank + 3 * cols] = exact(applied, applied, NT)
-        packed[:, rank + 3 * cols : rank + 4 * cols] = exact(residual, applied, NT)
+        packed[:, rank + 2 * cols : rank + 3 * cols] = found[cols : 2 * cols]
+        packed[:, rank + 3 * cols : rank + 4 * cols] = found[2 * cols :]
         write_halves(where_ref, packed, mine_ref, theirs_ref)
 
     return call(

time: 419 us -> 415 us (level)
  Pallas kernels: 205 us -> 200 us
    pallas_call x22, Pallas kernels: 205 us -> 200 us  [call(): pl.pallas_call(body, out_shape=[jax.ShapeDtypeStruct(shape, dtype) for sh...]
  transfers between devices with their start and end apart: 84 -> 84, of which waited for: 53 -> 53; matrix products, arithmetic and copies ran while one was open for 2% -> 2% of each run, Pallas kernels for 15% -> 14%
where the time goes in v3:
time: 415 us; the launch traced here: 414 us
  Pallas kernels  200 us (48%)
  starting transfers between devices  93.4 us (23%)
  waiting for transfers between devices  88.9 us (21%)
  other arithmetic  14.9 us (4%)
  local copies, waits for them, and re-layouts  14.8 us (4%)
    pallas_call x22, Pallas kernels, call(): pl.pallas_call(body, out_shape=[jax.ShapeDtypeStruct(shape, dtype) for sh...  200 us
    ppermute x84, starting transfers between devices, exchange(): return lax.ppermute(values, axis, [(at, at ^ mask) for at in range(size)])  93.4 us
    ppermute x84, waiting for transfers between devices, exchange(): return lax.ppermute(values, axis, [(at, at ^ mask) for at in range(size)])  88.9 us
  transfers between devices with their start and end apart: 84, of which 53 were waited for; matrix products, arithmetic and copies ran while one was open for 2% of the time, Pallas kernels for 14%

profile of v3, /device:TPU:0, one launch (start us, length us, event | category | flops | bytes accessed | tf_op | source)
XLA Modules:
  0.0 414.2 jit_solution(1192833584228774582)
XLA Ops:
  5.7 4.5 %shard_map.59 = f32[64,128]{1,0:T(8,128)} custom-call(s32[3]{0:T(128)} %pad_add_fusion.where_ref, f32[32,8192]{1,0:T(8,128)} %bitcast.99, f32[32,8192]{1,0:T(8,128)} %copy-done.11, bf16[8192,384]{1,0:T(8,128)(2,1)} %factor_ref.1), custom_call_target="tpu_custom_call" | custom-call | tf_op jit(solution)/shard_map/pallas_call | solution.py:36
  10.2 3.1 collective-permute-start.1
  48.0 17.8 %shard_map.62 = (bf16[64,1024]{1,0:T(8,128)(2,1)S(1)}, bf16[64,1024]{1,0:T(8,128)(2,1)S(1)}, bf16[64,1024]{1,0:T(8,128)(2,1)S(1)}) custom-call(s32[3]{0:T(128)S(1)} %copy-done.7, bf16[4096,8192]{1,0:T(8,128)(2,1)} %design_ref.23, bf16[4,64,1024]{2,1,0:T(8,128)(2,1)S(1)} %pad_maximum_fusion.refs_0_, bf16[4,64,1024]{2,1,0:T(8,128)(2,1)S(1)} %collective-permute-done.12.refs_1_), custom_call_target="tpu_custom_call" | custom-call | flops 3221225472 | bytes 50331648 | tf_op jit(solution)/shard_map/pallas_call | solution.py:36
  66.3 3.9 collective-permute-start.15
  70.2 7.8 %shard_map.61 = bf16[64,1024]{1,0:T(8,128)(2,1)S(1)} custom-call(s32[3]{0:T(128)S(1)} %copy-done.7, bf16[4096,8192]{1,0:T(8,128)(2,1)} %design_ref.23, bf16[4,64,1024]{2,1,0:T(8,128)(2,1)S(1)} %pad_maximum_fusion.refs_0_, bf16[4,64,1024]{2,1,0:T(8,128)(2,1)S(1)} %collective-permute-done.12.refs_1_), custom_call_target="tpu_custom_call" | custom-call | flops 1073741824 | bytes 16777216 | tf_op jit(solution)/shard_map/pallas_call | solution.py:36
  82.6 6.9 %shard_map.63.refs_3_ = f32[64,8192]{1,0:T(8,128)S(1)} custom-call(s32[3]{0:T(128)S(1)} %copy-done.7, bf16[4096,8192]{1,0:T(8,128)(2,1)} %design_ref.23, bf16[64,1024]{1,0:T(8,128)(2,1)S(1)} %add_convert_fusion.10.refs_0_), custom_call_target="tpu_custom_call" | custom-call | flops 1073741824 | bytes 16777216 | tf_op jit(solution)/shard_map/pallas_call | solution.py:36
  90.8 16.8 %shard_map.64 = (bf16[4,64,1024]{2,1,0:T(8,128)(2,1)S(1)}, bf16[4,64,1024]{2,1,0:T(8,128)(2,1)S(1)}) custom-call(s32[3]{0:T(128)S(1)} %copy-done.7, bf16[4096,8192]{1,0:T(8,128)(2,1)} %design_ref.23, bf16[64,1024]{1,0:T(8,128)(2,1)S(1)} %collective-permute-done.16.refs_0_, bf16[64,1024]{1,0:T(8,128)(2,1)S(1)} %collective-permute-done.17.refs_1_, ...), custom_call_target="tpu_custom_call" | custom-call | flops 3221225472 | bytes 50331648 | tf_op jit(solution)/shard_map/pallas_call | solution.py:36
  116.5 3.6 collective-permute-done.21.refs_1_
  120.7 3.8 shard_map.65
  152.5 10.5 %shard_map.66 = (f32[64,64]{1,0:T(8,128)}, f32[64,1024]{1,0:T(8,128)}, f32[64,768]{1,0:T(8,128)}, f32[64,1024]{1,0:T(8,128)}, bf16[64,1024]{1,0:T(8,128)(2,1)}) custom-call(s32[3]{0:T(128)} %pad_add_fusion.where_ref, f32[4,64,128]{2,1,0:T(8,128)} %copy-done.13, f32[4,64,128]{2,1,0:T(8,128)} %copy-done.25, f32[64,768]{1,0:T(8,128)} %get-tuple-element.48.refs_2_, ...), custom_call_target="tpu_custom_call" | custom-call | tf_op jit(solution)/shard_map/pallas_call | solution.py:36
  166.5 3.1 collective-permute-done.34
  174.8 17.8 %shard_map.68 = (bf16[64,1024]{1,0:T(8,128)(2,1)S(1)}, bf16[64,1024]{1,0:T(8,128)(2,1)S(1)}, bf16[64,1024]{1,0:T(8,128)(2,1)S(1)}) custom-call(s32[3]{0:T(128)S(1)} %copy-done.8, bf16[4096,8192]{1,0:T(8,128)(2,1)} %design_ref.23, bf16[4,64,1024]{2,1,0:T(8,128)(2,1)S(1)} %pad_maximum_fusion.1.refs_0_.refs_2_, ...), custom_call_target="tpu_custom_call" | custom-call | flops 3221225472 | bytes 50331648 | tf_op jit(solution)/shard_map/pallas_call | solution.py:36
  197.1 7.8 %shard_map.67 = bf16[64,1024]{1,0:T(8,128)(2,1)S(1)} custom-call(s32[3]{0:T(128)S(1)} %copy-done.8, bf16[4096,8192]{1,0:T(8,128)(2,1)} %design_ref.23, bf16[4,64,1024]{2,1,0:T(8,128)(2,1)S(1)} %pad_maximum_fusion.1.refs_0_.refs_2_, bf16[4,64,1024]{2,1,0:T(8,128)(2,1)S(1)} %collective-permute-done.37.refs_1_.refs_3_), custom_call_target="tpu_custom_call" | custom-call | flops 1073741824 | bytes 16777216 | tf_op jit(solution)/shard_map/pallas_call | solution.py:36
  210.8 6.9 %shard_map.69.refs_3_ = f32[64,8192]{1,0:T(8,128)S(1)} custom-call(s32[3]{0:T(128)S(1)} %copy-done.8, bf16[4096,8192]{1,0:T(8,128)(2,1)} %design_ref.23, bf16[64,1024]{1,0:T(8,128)(2,1)S(1)} %add_convert_fusion.6.refs_0_), custom_call_target="tpu_custom_call" | custom-call | flops 1073741824 | bytes 16777216 | tf_op jit(solution)/shard_map/pallas_call | solution.py:36
  219.3 16.8 %shard_map.70 = (bf16[4,64,1024]{2,1,0:T(8,128)(2,1)S(1)}, bf16[4,64,1024]{2,1,0:T(8,128)(2,1)S(1)}) custom-call(s32[3]{0:T(128)S(1)} %copy-done.8, bf16[4096,8192]{1,0:T(8,128)(2,1)} %design_ref.23, bf16[64,1024]{1,0:T(8,128)(2,1)S(1)} %collective-permute-done.41.refs_0_, bf16[64,1024]{1,0:T(8,128)(2,1)S(1)} %collective-permute-done.42.refs_1_, ...), custom_call_target="tpu_custom_call" | custom-call | flops 3221225472 | bytes 50331648 | tf_op jit(solution)/shard_map/pallas_call | solution.py:36
  244.9 3.6 collective-permute-done.46.refs_1_
  249.2 3.8 shard_map.71
  280.1 10.4 %shard_map.72 = (f32[64,64]{1,0:T(8,128)}, f32[64,1024]{1,0:T(8,128)}, f32[64,768]{1,0:T(8,128)}, f32[64,1024]{1,0:T(8,128)}, bf16[64,1024]{1,0:T(8,128)(2,1)}) custom-call(s32[3]{0:T(128)} %pad_add_fusion.where_ref, f32[4,64,128]{2,1,0:T(8,128)} %copy-done.12, f32[4,64,128]{2,1,0:T(8,128)} %copy-done.24, f32[64,768]{1,0:T(8,128)} %get-tuple-element.60.refs_2_, ...), custom_call_target="tpu_custom_call" | custom-call | tf_op jit(solution)/shard_map/pallas_call | solution.py:36
  302.3 17.8 %shard_map.74 = (bf16[64,1024]{1,0:T(8,128)(2,1)S(1)}, bf16[64,1024]{1,0:T(8,128)(2,1)S(1)}, bf16[64,1024]{1,0:T(8,128)(2,1)S(1)}) custom-call(s32[3]{0:T(128)S(1)} %copy-done.9, bf16[4096,8192]{1,0:T(8,128)(2,1)} %design_ref.23, bf16[4,64,1024]{2,1,0:T(8,128)(2,1)S(1)} %pad_maximum_fusion.2.refs_0_.refs_4_, ...), custom_call_target="tpu_custom_call" | custom-call | flops 3221225472 | bytes 50331648 | tf_op jit(solution)/shard_map/pallas_call | solution.py:36
  324.6 7.8 %shard_map.73.kept_ref = bf16[64,1024]{1,0:T(8,128)(2,1)S(1)} custom-call(s32[3]{0:T(128)S(1)} %copy-done.9, bf16[4096,8192]{1,0:T(8,128)(2,1)} %design_ref.23, bf16[4,64,1024]{2,1,0:T(8,128)(2,1)S(1)} %pad_maximum_fusion.2.refs_0_.refs_4_, bf16[4,64,1024]{2,1,0:T(8,128)(2,1)S(1)} %collective-permute-done.62.refs_1_.refs_5_), custom_call_target="tpu_custom_call" | custom-call | flops 1073741824 | bytes 16777216 | tf_op jit(solution)/shard_map/pallas_call | solution.py:36
  342.5 6.9 %shard_map.78.refs_3_ = f32[64,8192]{1,0:T(8,128)S(1)} custom-call(s32[3]{0:T(128)S(1)} %copy-done.9, bf16[4096,8192]{1,0:T(8,128)(2,1)} %design_ref.23, bf16[64,1024]{1,0:T(8,128)(2,1)S(1)} %copy-done.10), custom_call_target="tpu_custom_call" | custom-call | flops 1073741824 | bytes 16777216 | tf_op jit(solution)/shard_map/pallas_call | solution.py:36
  350.4 17.0 %shard_map.79 = (bf16[4,64,1024]{2,1,0:T(8,128)(2,1)S(1)}, bf16[4,64,1024]{2,1,0:T(8,128)(2,1)S(1)}) custom-call(s32[3]{0:T(128)S(1)} %copy-done.9, bf16[4096,8192]{1,0:T(8,128)(2,1)} %design_ref.23, bf16[64,1024]{1,0:T(8,128)(2,1)S(1)} %collective-permute-done.73.refs_0_, bf16[64,1024]{1,0:T(8,128)(2,1)S(1)} %collective-permute-done.74.refs_1_, ...), custom_call_target="tpu_custom_call" | custom-call | flops 3221225472 | bytes 50331648 | tf_op jit(solution)/shard_map/pallas_call | solution.py:36
  388.3 7.3 %shard_map.76.refs_8_.refs_5_ = f32[64,64]{1,0:T(8,128)} custom-call(f32[64,128]{1,0:T(8,128)} %add.283.gram_ref), custom_call_target="tpu_custom_call" | custom-call | flops 1000000000 | tf_op jit(solution)/shard_map/pallas_call | solution.py:36
  404.6 3.8 shard_map.77
  (271 shorter events, 202.8 us)
Async XLA Ops:
  2.7 23.4 %collective-permute-start.8 = (bf16[1024,384]{1,0:T(8,128)(2,1)S(1)}, bf16[1024,384]{1,0:T(8,128)(2,1)S(1)}, u32[]{:S(2)}, u32[]{:S(2)}) collective-permute-start(bf16[1024,384]{1,0:T(8,128)(2,1)S(1)} %get-tuple-element.77), channel_id=1, source_target_pairs={{0,1},{1,0},{2,3},{3,2},{4,5},{5,4},{6,7},{7,6},{8,9},{9,8},{10,11... | collective-permute-start | bytes 2359304 | tf_op jit(solution)/shard_map/ppermute | solution.py:48
  36.3 8.6 %collective-permute-start.10 = (bf16[64,1024]{1,0:T(8,128)(2,1)}, bf16[64,1024]{1,0:T(8,128)(2,1)S(1)}, u32[]{:S(2)}, u32[]{:S(2)}) collective-permute-start(bf16[64,1024]{1,0:T(8,128)(2,1)} %get-tuple-element.39), channel_id=1, source_target_pairs={{0,16},{8,24},{16,0},{24,8},{1,17},{9,25},{17,1},{25,9},{2,18},{10... | collective-permute-start | bytes 393224 | tf_op jit(solution)/shard_map/ppermute | solution.py:48
  65.8 12.2 %collective-permute-start.13 = (bf16[64,1024]{1,0:T(8,128)(2,1)S(1)}, bf16[64,1024]{1,0:T(8,128)(2,1)S(1)}, u32[]{:S(2)}, u32[]{:S(2)}) collective-permute-start(bf16[64,1024]{1,0:T(8,128)(2,1)S(1)} %get-tuple-element.40), channel_id=1, source_target_pairs={{0,6},{2,4},{4,2},{6,0},{1,7},{3,5},{5,3},{7,1},{8,14},{10,12},{12... | collective-permute-start | bytes 393224 | tf_op jit(solution)/shard_map/ppermute | solution.py:48
  66.3 11.8 %collective-permute-start.14 = (bf16[64,1024]{1,0:T(8,128)(2,1)S(1)}, bf16[64,1024]{1,0:T(8,128)(2,1)S(1)}, u32[]{:S(2)}, u32[]{:S(2)}) collective-permute-start(bf16[64,1024]{1,0:T(8,128)(2,1)S(1)} %get-tuple-element.41), channel_id=1, source_target_pairs={{0,4},{2,6},{4,0},{6,2},{1,5},{3,7},{5,1},{7,3},{8,12},{10,14},{12... | collective-permute-start | bytes 393224 | tf_op jit(solution)/shard_map/ppermute | solution.py:48
  66.3 11.8 %collective-permute-start.15 = (bf16[64,1024]{1,0:T(8,128)(2,1)S(1)}, bf16[64,1024]{1,0:T(8,128)(2,1)S(1)}, u32[]{:S(2)}, u32[]{:S(2)}) collective-permute-start(bf16[64,1024]{1,0:T(8,128)(2,1)S(1)} %get-tuple-element.42), channel_id=1, source_target_pairs={{0,2},{2,0},{4,6},{6,4},{1,3},{3,1},{5,7},{7,5},{8,10},{10,8},{12,... | collective-permute-start | bytes 393224 | tf_op jit(solution)/shard_map/ppermute | solution.py:48
  78.2 11.4 %collective-permute-start.16 = (bf16[64,1024]{1,0:T(8,128)(2,1)S(1)}, bf16[64,1024]{1,0:T(8,128)(2,1)S(1)}, u32[]{:S(2)}, u32[]{:S(2)}) collective-permute-start(bf16[64,1024]{1,0:T(8,128)(2,1)S(1)} %add_convert_fusion.10.refs_0_), channel_id=1, source_target_pairs={{0,2},{2,0},{4,6},{6,4},{1,3},{3,1},{5,7},{7,5},{8,10},{10,8},{12,... | collective-permute-start | bytes 393224 | tf_op jit(solution)/shard_map/ppermute | solution.py:48
  78.2 12.6 %collective-permute-start.17 = (bf16[64,1024]{1,0:T(8,128)(2,1)S(1)}, bf16[64,1024]{1,0:T(8,128)(2,1)S(1)}, u32[]{:S(2)}, u32[]{:S(2)}) collective-permute-start(bf16[64,1024]{1,0:T(8,128)(2,1)S(1)} %add_convert_fusion.10.refs_0_), channel_id=1, source_target_pairs={{0,4},{2,6},{4,0},{6,2},{1,5},{3,7},{5,1},{7,3},{8,12},{10,14},{12... | collective-permute-start | bytes 393224 | tf_op jit(solution)/shard_map/ppermute | solution.py:48
  81.0 9.8 %collective-permute-start.18 = (bf16[64,1024]{1,0:T(8,128)(2,1)S(1)}, bf16[64,1024]{1,0:T(8,128)(2,1)S(1)}, u32[]{:S(2)}, u32[]{:S(2)}) collective-permute-start(bf16[64,1024]{1,0:T(8,128)(2,1)S(1)} %add_convert_fusion.10.refs_0_), channel_id=1, source_target_pairs={{0,6},{2,4},{4,2},{6,0},{1,7},{3,5},{5,3},{7,1},{8,14},{10,12},{12... | collective-permute-start | bytes 393224 | tf_op jit(solution)/shard_map/ppermute | solution.py:48
  192.6 12.2 %collective-permute-start.38 = (bf16[64,1024]{1,0:T(8,128)(2,1)S(1)}, bf16[64,1024]{1,0:T(8,128)(2,1)S(1)}, u32[]{:S(2)}, u32[]{:S(2)}) collective-permute-start(bf16[64,1024]{1,0:T(8,128)(2,1)S(1)} %get-tuple-element.51), channel_id=1, source_target_pairs={{0,6},{2,4},{4,2},{6,0},{1,7},{3,5},{5,3},{7,1},{8,14},{10,12},{12... | collective-permute-start | bytes 393224 | tf_op jit(solution)/shard_map/ppermute | solution.py:48
  194.1 12.2 %collective-permute-start.39 = (bf16[64,1024]{1,0:T(8,128)(2,1)S(1)}, bf16[64,1024]{1,0:T(8,128)(2,1)S(1)}, u32[]{:S(2)}, u32[]{:S(2)}) collective-permute-start(bf16[64,1024]{1,0:T(8,128)(2,1)S(1)} %get-tuple-element.52), channel_id=1, source_target_pairs={{0,4},{2,6},{4,0},{6,2},{1,5},{3,7},{5,1},{7,3},{8,12},{10,14},{12... | collective-permute-start | bytes 393224 | tf_op jit(solution)/shard_map/ppermute | solution.py:48
  194.3 12.0 %collective-permute-start.40 = (bf16[64,1024]{1,0:T(8,128)(2,1)S(1)}, bf16[64,1024]{1,0:T(8,128)(2,1)S(1)}, u32[]{:S(2)}, u32[]{:S(2)}) collective-permute-start(bf16[64,1024]{1,0:T(8,128)(2,1)S(1)} %get-tuple-element.53), channel_id=1, source_target_pairs={{0,2},{2,0},{4,6},{6,4},{1,3},{3,1},{5,7},{7,5},{8,10},{10,8},{12,... | collective-permute-start | bytes 393224 | tf_op jit(solution)/shard_map/ppermute | solution.py:48
  206.3 11.4 %collective-permute-start.41 = (bf16[64,1024]{1,0:T(8,128)(2,1)S(1)}, bf16[64,1024]{1,0:T(8,128)(2,1)S(1)}, u32[]{:S(2)}, u32[]{:S(2)}) collective-permute-start(bf16[64,1024]{1,0:T(8,128)(2,1)S(1)} %add_convert_fusion.6.refs_0_), channel_id=1, source_target_pairs={{0,2},{2,0},{4,6},{6,4},{1,3},{3,1},{5,7},{7,5},{8,10},{10,8},{12,... | collective-permute-start | bytes 393224 | tf_op jit(solution)/shard_map/ppermute | solution.py:48
  206.4 12.8 %collective-permute-start.42 = (bf16[64,1024]{1,0:T(8,128)(2,1)S(1)}, bf16[64,1024]{1,0:T(8,128)(2,1)S(1)}, u32[]{:S(2)}, u32[]{:S(2)}) collective-permute-start(bf16[64,1024]{1,0:T(8,128)(2,1)S(1)} %add_convert_fusion.6.refs_0_), channel_id=1, source_target_pairs={{0,4},{2,6},{4,0},{6,2},{1,5},{3,7},{5,1},{7,3},{8,12},{10,14},{12... | collective-permute-start | bytes 393224 | tf_op jit(solution)/shard_map/ppermute | solution.py:48
  208.4 10.9 %collective-permute-start.43 = (bf16[64,1024]{1,0:T(8,128)(2,1)S(1)}, bf16[64,1024]{1,0:T(8,128)(2,1)S(1)}, u32[]{:S(2)}, u32[]{:S(2)}) collective-permute-start(bf16[64,1024]{1,0:T(8,128)(2,1)S(1)} %add_convert_fusion.6.refs_0_), channel_id=1, source_target_pairs={{0,6},{2,4},{4,2},{6,0},{1,7},{3,5},{5,3},{7,1},{8,14},{10,12},{12... | collective-permute-start | bytes 393224 | tf_op jit(solution)/shard_map/ppermute | solution.py:48
  320.1 12.9 %collective-permute-start.63 = (bf16[64,1024]{1,0:T(8,128)(2,1)S(1)}, bf16[64,1024]{1,0:T(8,128)(2,1)S(1)}, u32[]{:S(2)}, u32[]{:S(2)}) collective-permute-start(bf16[64,1024]{1,0:T(8,128)(2,1)S(1)} %get-tuple-element.65), channel_id=1, source_target_pairs={{0,6},{2,4},{4,2},{6,0},{1,7},{3,5},{5,3},{7,1},{8,14},{10,12},{12... | collective-permute-start | bytes 393224 | tf_op jit(solution)/shard_map/ppermute | solution.py:48
  322.6 11.2 %collective-permute-start.64 = (bf16[64,1024]{1,0:T(8,128)(2,1)S(1)}, bf16[64,1024]{1,0:T(8,128)(2,1)S(1)}, u32[]{:S(2)}, u32[]{:S(2)}) collective-permute-start(bf16[64,1024]{1,0:T(8,128)(2,1)S(1)} %get-tuple-element.66), channel_id=1, source_target_pairs={{0,4},{2,6},{4,0},{6,2},{1,5},{3,7},{5,1},{7,3},{8,12},{10,14},{12... | collective-permute-start | bytes 393224 | tf_op jit(solution)/shard_map/ppermute | solution.py:48
  322.6 11.2 %collective-permute-start.65 = (bf16[64,1024]{1,0:T(8,128)(2,1)S(1)}, bf16[64,1024]{1,0:T(8,128)(2,1)S(1)}, u32[]{:S(2)}, u32[]{:S(2)}) collective-permute-start(bf16[64,1024]{1,0:T(8,128)(2,1)S(1)} %get-tuple-element.67), channel_id=1, source_target_pairs={{0,2},{2,0},{4,6},{6,4},{1,3},{3,1},{5,7},{7,5},{8,10},{10,8},{12,... | collective-permute-start | bytes 393224 | tf_op jit(solution)/shard_map/ppermute | solution.py:48
  337.2 12.3 %collective-permute-start.73 = (bf16[64,1024]{1,0:T(8,128)(2,1)}, bf16[64,1024]{1,0:T(8,128)(2,1)S(1)}, u32[]{:S(2)}, u32[]{:S(2)}) collective-permute-start(bf16[64,1024]{1,0:T(8,128)(2,1)} %get-tuple-element.71.refs_0_), channel_id=1, source_target_pairs={{0,2},{2,0},{4,6},{6,4},{1,3},{3,1},{5,7},{7,5},{8,10},{10,8},{12,... | collective-permute-start | bytes 393224 | tf_op jit(solution)/shard_map/ppermute | solution.py:48
  337.2 13.2 %collective-permute-start.74 = (bf16[64,1024]{1,0:T(8,128)(2,1)}, bf16[64,1024]{1,0:T(8,128)(2,1)S(1)}, u32[]{:S(2)}, u32[]{:S(2)}) collective-permute-start(bf16[64,1024]{1,0:T(8,128)(2,1)} %get-tuple-element.71.refs_0_), channel_id=1, source_target_pairs={{0,4},{2,6},{4,0},{6,2},{1,5},{3,7},{5,1},{7,3},{8,12},{10,14},{12... | collective-permute-start | bytes 393224 | tf_op jit(solution)/shard_map/ppermute | solution.py:48
  340.2 10.2 %collective-permute-start.75 = (bf16[64,1024]{1,0:T(8,128)(2,1)}, bf16[64,1024]{1,0:T(8,128)(2,1)S(1)}, u32[]{:S(2)}, u32[]{:S(2)}) collective-permute-start(bf16[64,1024]{1,0:T(8,128)(2,1)} %get-tuple-element.71.refs_0_), channel_id=1, source_target_pairs={{0,6},{2,4},{4,2},{6,0},{1,7},{3,5},{5,3},{7,1},{8,14},{10,12},{12... | collective-permute-start | bytes 393224 | tf_op jit(solution)/shard_map/ppermute | solution.py:48
  367.4 15.8 %collective-permute-start.76 = (bf16[4,64,1024]{2,1,0:T(8,128)(2,1)S(1)}, bf16[4,64,1024]{2,1,0:T(8,128)(2,1)S(1)}, u32[]{:S(2)}, u32[]{:S(2)}) collective-permute-start(bf16[4,64,1024]{2,1,0:T(8,128)(2,1)S(1)} %get-tuple-element.73), channel_id=1, source_target_pairs={{0,1},{1,0},{2,3},{3,2},{4,5},{5,4},{6,7},{7,6},{8,9},{9,8},{10,11... | collective-permute-start | bytes 1572872 | tf_op jit(solution)/shard_map/ppermute | solution.py:48
  384.2 11.4 %collective-permute-start.77 = (bf16[64,1024]{1,0:T(8,128)(2,1)S(1)}, bf16[64,1024]{1,0:T(8,128)(2,1)S(1)}, u32[]{:S(2)}, u32[]{:S(2)}) collective-permute-start(bf16[64,1024]{1,0:T(8,128)(2,1)S(1)} %get-tuple-element.80), channel_id=1, source_target_pairs={{0,8},{8,0},{16,24},{24,16},{1,9},{9,1},{17,25},{25,17},{2,10},{10... | collective-permute-start | bytes 393224 | tf_op jit(solution)/shard_map/ppermute | solution.py:48
  385.4 10.2 %collective-permute-start.78 = (bf16[64,1024]{1,0:T(8,128)(2,1)S(1)}, bf16[64,1024]{1,0:T(8,128)(2,1)S(1)}, u32[]{:S(2)}, u32[]{:S(2)}) collective-permute-start(bf16[64,1024]{1,0:T(8,128)(2,1)S(1)} %get-tuple-element.79), channel_id=1, source_target_pairs={{0,16},{8,24},{16,0},{24,8},{1,17},{9,25},{17,1},{25,9},{2,18},{10... | collective-permute-start | bytes 393224 | tf_op jit(solution)/shard_map/ppermute | solution.py:48
  386.2 9.4 %collective-permute-start.79 = (bf16[64,1024]{1,0:T(8,128)(2,1)S(1)}, bf16[64,1024]{1,0:T(8,128)(2,1)S(1)}, u32[]{:S(2)}, u32[]{:S(2)}) collective-permute-start(bf16[64,1024]{1,0:T(8,128)(2,1)S(1)} %get-tuple-element.78), channel_id=1, source_target_pairs={{0,24},{8,16},{16,8},{24,0},{1,25},{9,17},{17,9},{25,1},{2,26},{10... | collective-permute-start | bytes 393224 | tf_op jit(solution)/shard_map/ppermute | solution.py:48
  (92 other events, 556.4 us)
